TPU v7x, 32 devices: a whole 2x2x4 slice. The times are simulated.
32 devices in a mesh: shift: 8 (over y, x, core), dom: 4 (over z).
Axes of the slice: x: 2, y: 2, z: 4, core: 2. Of those that a mesh axis runs over, the one named last changes fastest.
Arguments:
- samples: float32 [32, 64, 1024], P('dom'), may hold values from -6 to 6
- potential: float32 [32, 1024], P('dom'), may hold values from 0 to 4
Outputs:
- subspace: float32 [32, 64, 1024], P('dom')
- reduced_h: float32 [64, 64], replicated
- reduced_b: float32 [64, 64], replicated
All inputs are finite; a program needn't handle non-finite values.
Results may differ from a plain program's by a relative error of at most 0.00027.
Values sent between devices are 32-bit elements; how exact they have to be, the bound alone decides.
No kernel may reach another device: no remote copies, remote signals or barrier semaphores. Data moves between devices by JAX's collectives and lax.ppermute only.
A program may use at most 128 MiB of HBM per device.

v0:
```python
import jax
import jax.numpy as jnp
from jax import lax
from jax.sharding import PartitionSpec as P

NX = 32
NY = 32


CENTRE = 3.0
RADIUS = 2.0
RIDGE = 0.01


def extended_2(x, sides, width):
    for axis, dim in sides:
        count, length = (lax.axis_size(axis), x.shape[dim])
        up = [(i, (i + 1) % count) for i in range(count - 1)]
        down = [(j, i) for i, j in up]
        last = lax.slice_in_dim(x, length - width, length, axis=dim)
        first = lax.slice_in_dim(x, 0, width, axis=dim)
        before = lax.ppermute(last, axis, up)
        after = lax.ppermute(first, axis, down)
        x = jnp.concatenate([before, x, after], axis=dim)
    return x


def plane_sum(values):
    extent = values.shape[-1]
    leading = [(0, 0)] * (values.ndim - 1)
    padded = jnp.pad(values, leading + [(NY, NY)])
    column = lax.broadcasted_iota(jnp.int32, (extent,), 0) % NY
    lower_ok = (column != 0).astype(values.dtype)
    upper_ok = (column != NY - 1).astype(values.dtype)
    return (
        padded[..., 0:extent]
        + padded[..., 2 * NY : 2 * NY + extent]
        + padded[..., NY - 1 : NY - 1 + extent] * lower_ok
        + padded[..., NY + 1 : NY + 1 + extent] * upper_ok
    )


def colsum(values):
    return jnp.sum(values, axis=(0, 2))


def on_device(samples, potential):
    nodes = lax.axis_size("shift")
    planes = samples.shape[0]
    order = lax.axis_index("shift").astype(jnp.float32)
    angle = jnp.pi * (order + 0.5) / nodes
    shift_re = CENTRE + RADIUS * jnp.cos(angle)
    shift_im = RADIUS * jnp.sin(angle)
    weight_re = RADIUS * jnp.cos(angle) / nodes
    weight_im = RADIUS * jnp.sin(angle) / nodes

    def inverses(onsite_part):
        diag_re = shift_re - onsite_part
        modulus = diag_re * diag_re + shift_im * shift_im
        return (diag_re / modulus, -shift_im / modulus)

    def apply_inv(vector, inv_pair):
        return jnp.stack(
            [
                vector[0] * inv_pair[0] - vector[1] * inv_pair[1],
                vector[0] * inv_pair[1] + vector[1] * inv_pair[0],
            ]
        )

    def combine(vector, hamil):
        return jnp.stack(
            [
                shift_re * vector[0] - shift_im * vector[1] - hamil[0],
                shift_re * vector[1] + shift_im * vector[0] - hamil[1],
            ]
        )

    onsite = (6.0 + potential)[:, None, :]
    inv_own = inverses(onsite)

    def shrink_operate(vector, onsite_inner):
        inner = vector[:, 1:-1]
        beside = vector[:, 2:] + vector[:, :-2] + plane_sum(inner)
        return combine(inner, onsite_inner * inner - beside)

    joined = jnp.concatenate([samples, potential[:, None, :]], axis=1)
    extended = extended_2(joined, (("dom", 0),), 2)
    ext_samples = extended[:, :-1]
    ext_onsite = 6.0 + extended[:, -1:]
    inv_ext = inverses(ext_onsite)
    first_ext = apply_inv(jnp.stack([ext_samples, jnp.zeros_like(ext_samples)]), inv_ext)
    image_ext = shrink_operate(first_ext, ext_onsite[1:-1])
    total_planes = planes * lax.axis_size("dom")
    plane_index = (
        lax.axis_index("dom") * planes - 1 + lax.broadcasted_iota(jnp.int32, (planes + 2,), 0)
    )
    inside = ((plane_index >= 0) & (plane_index < total_planes)).astype(jnp.float32)
    image_ext = image_ext * inside[None, :, None, None]
    image_one = image_ext[:, 1:-1]
    first_block_real = image_one[0]
    first_block_imag = image_one[1]
    first_set = jnp.stack(
        [
            colsum(first_block_real * first_block_real + first_block_imag * first_block_imag),
            colsum(first_block_real * samples),
            colsum(-first_block_imag * samples),
        ]
    )
    first_tot = lax.psum(first_set, "dom")
    inv_mid = (inv_ext[0][1:-1], inv_ext[1][1:-1])
    image_two = shrink_operate(apply_inv(image_ext, inv_mid), ext_onsite[2:-2])
    two_re = image_two[0]
    two_im = image_two[1]
    second_set = jnp.stack(
        [
            colsum(first_block_real * two_re + first_block_imag * two_im),
            colsum(first_block_real * two_im - first_block_imag * two_re),
            colsum(two_re * two_re + two_im * two_im),
            colsum(two_re * samples),
            colsum(-two_im * samples),
        ]
    )
    second_tot = lax.psum(second_set, "dom")
    totals = jnp.concatenate([first_tot, second_tot], axis=0)
    g_one = totals[0]
    q_one_re = totals[1]
    q_one_im = totals[2]
    g_mix_re = totals[3]
    g_mix_im = totals[4]
    g_two = totals[5]
    q_two_re = totals[6]
    q_two_im = totals[7]
    ridge = RIDGE * (g_one + g_two) / 2.0
    determ = (g_one + ridge) * (g_two + ridge) - (g_mix_re * g_mix_re + g_mix_im * g_mix_im)
    coef_one_re = (
        (g_two + ridge) * q_one_re - (g_mix_re * q_two_re - g_mix_im * q_two_im)
    ) / determ
    coef_one_im = (
        (g_two + ridge) * q_one_im - (g_mix_re * q_two_im + g_mix_im * q_two_re)
    ) / determ
    coef_two_re = (
        (g_one + ridge) * q_two_re - (g_mix_re * q_one_re + g_mix_im * q_one_im)
    ) / determ
    coefficient_second_imag = (
        (g_one + ridge) * q_two_im - (g_mix_re * q_one_im - g_mix_im * q_one_re)
    ) / determ
    first_coefficient_real = coef_one_re[None, :, None]
    first_coefficient_imag = coef_one_im[None, :, None]
    second_coefficient_real = coef_two_re[None, :, None]
    second_coefficient_imag = coefficient_second_imag[None, :, None]
    solution = apply_inv(
        jnp.stack(
            [
                first_coefficient_real * samples
                + second_coefficient_real * first_block_real
                - second_coefficient_imag * first_block_imag,
                first_coefficient_imag * samples
                + second_coefficient_real * first_block_imag
                + second_coefficient_imag * first_block_real,
            ]
        ),
        inv_own,
    )
    weighted = weight_re * solution[0] - weight_im * solution[1]
    scale = 1.0 / (NX * NY * planes * lax.axis_size("dom"))
    subspace = lax.psum(weighted, "shift")
    padded = extended_2(subspace, (("dom", 0),), 1)
    applied = onsite * subspace - (padded[2:] + padded[:-2] + plane_sum(subspace))
    part_h = jnp.einsum("znc,zmc->nm", subspace, applied, precision=lax.Precision.HIGHEST) * scale
    part_b = jnp.einsum("znc,zmc->nm", subspace, subspace, precision=lax.Precision.HIGHEST) * scale
    reduced_h, reduced_b = lax.psum((part_h, part_b), "dom")
    return (subspace, reduced_h, reduced_b)


def solution(mesh):
    in_specs = (P("dom", None, None), P("dom", None))
    out_specs = (P("dom", None, None), P(), P())
    return jax.shard_map(
        on_device, mesh=mesh, in_specs=in_specs, out_specs=out_specs, check_vma=False
    )
```

profile of v0, /device:TPU:0, one launch (start us, length us, event | category | flops | bytes accessed | tf_op | source)
XLA Modules:
  0.0 185.9 jit_solution(1204473247824905076)
XLA Ops:
  7.2 1.7 constant_dynamic-update-slice_fusion
  9.2 0.4 copy.8
  9.7 5.0 %collective-permute-start = (f32[2,65,1024]{2,0,1:T(2,128)S(1)}, f32[2,65,1024]{2,0,1:T(2,128)S(1)}, u32[]{:S(2)}, u32[]{:S(2)}) collective-permute-start(f32[2,65,1024]{2,0,1:T(2,128)S(1)} %copy.8), channel_id=1, source_target_pairs={{0,1},{1,2},{2,3},{4,5},{5,6},{6,7},{8,9},{9,10},{10,11},{12,13},{... | collective-permute-start | bytes 1597448 | tf_op jit(solution)/shard_map/ppermute | solution.py:22
  14.7 1.2 copy.9
  15.9 1.3 collective-permute-start.1
  17.3 0.6 broadcast_add_fusion
  18.0 8.0 %collective-permute-done = f32[2,65,1024]{2,0,1:T(2,128)S(1)} collective-permute-done((f32[2,65,1024]{2,0,1:T(2,128)S(1)}, f32[2,65,1024]{2,0,1:T(2,128)S(1)}, u32[]{:S(2)}, u32[]{:S(2)}) %collective-permute-start) | collective-permute-done | bytes 532512 | tf_op jit(solution)/shard_map/ppermute | solution.py:22
  26.0 0.2 copy.10
  26.1 5.5 %collective-permute-done.1 = f32[2,65,1024]{2,0,1:T(2,128)} collective-permute-done((f32[2,65,1024]{2,0,1:T(2,128)}, f32[2,65,1024]{2,0,1:T(2,128)}, u32[]{:S(2)}, u32[]{:S(2)}) %collective-permute-start.1) | collective-permute-done | bytes 532512 | tf_op jit(solution)/shard_map/ppermute | solution.py:23
  31.6 1.2 copy.11
  33.1 0.3 pad_maximum_fusion.2
  33.4 0.2 copy-done.3
  33.7 0.9 add_bitcast_fusion
  34.6 2.8 %fusion.9 = f32[2,10,64,1024]{3,2,1,0:T(8,128)} fusion(f32[1,12,64,1024]{3,2,1,0:T(8,128)S(1)} %get-tuple-element.29, f32[1,12,64,1024]{3,2,1,0:T(8,128)S(1)} %get-tuple-element.28), kind=kLoop, calls=%fused_computation.21 | loop fusion | flops 1310720 | bytes 11534336 | tf_op jit(solution)/shard_map/stack | solution.py:63
  37.4 13.4 %fusion.4 = f32[2,10,64,1024]{3,2,1,0:T(8,128)} fusion(f32[2,10,64,1024]{3,2,1,0:T(8,128)} %fusion.9, f32[1,12,64,1024]{3,2,1,0:T(8,128)S(1)} %get-tuple-element.29, f32[1,12,64,1024]{3,2,1,0:T(8,128)S(1)} %get-tuple-element.28, f32[1024]{0:T(1024)S(1)} %get-tuple-element.45, f32[1024]{0:T(1024)S(1)} %get-tuple-element.44, f32[10,1024]{1,0:T(8,128)S(1)} %bitcast.188), kind=kLoop, calls=%fused_computation.16 | loop fusion | flops 14417920 | bytes 16826368 | tf_op jit(solution)/shard_map/sub | solution.py:84
  50.8 3.8 %slice_subtract_fusion.1 = (f32[1,10,64,1024]{3,2,1,0:T(8,128)S(1)}, f32[1,10,64,1024]{3,2,1,0:T(8,128)S(1)}) fusion(f32[2,10,64,1024]{3,2,1,0:T(8,128)} %fusion.4, f32[1,12,64,1024]{3,2,1,0:T(8,128)S(1)} %get-tuple-element.28, f32[1,12,64,1024]{3,2,1,0:T(8,128)S(1)} %get-tuple-element.29, f32[]{:T(128)S(6)} %mul.491, f32[]{:T(128)S(6)} %add_shard_map.3), kind=kLoop, calls=%fused_computation.43 | loop fusion | flops 5242880 | bytes 15728648 | tf_op jit(solution)/shard_map/sub | solution.py:73
  54.7 0.9 maximum_multiply_fusion
  55.6 1.3 multiply_add_fusion
  56.8 0.6 fusion.19
  57.4 4.8 %fusion.14 = f32[2,8,64,1024]{3,2,1,0:T(8,128)S(1)} fusion(f32[2,8,64,1024]{3,2,1,0:T(8,128)S(1)} %fusion.19, f32[1,10,64,1024]{3,2,1,0:T(8,128)S(1)} %get-tuple-element.27, f32[1,10,64,1024]{3,2,1,0:T(8,128)S(1)} %get-tuple-element.26, f32[1024]{0:T(1024)S(1)} %get-tuple-element.45, f32[1024]{0:T(1024)S(1)} %get-tuple-element.44, f32[8,1024]{1,0:T(8,128)S(1)} %bitcast.189), kind=kLoop, calls=%fused_computation.32 | loop fusion | flops 11534336 | bytes 13672448 | tf_op jit(solution)/shard_map/sub | solution.py:84
  62.3 1.5 fusion.36
  63.9 2.0 %multiply_reduce_fusion.1 = (f32[64]{0:T(128)S(1)}, f32[64]{0:T(128)S(1)}, f32[64]{0:T(128)S(1)}, f32[64]{0:T(128)S(1)}, f32[64]{0:T(128)S(1)}, /*index=5*/f32[64]{0:T(128)S(1)}, f32[64]{0:T(128)S(1)}, f32[64]{0:T(128)S(1)}) fusion(f32[8,64,1024]{2,1,0:T(8,128)S(1)} %copy-done.2, f32[2,10,64,1024]{3,2,1,0:T(8,128)S(1)} %maximum_multiply_fusion, ...), kind=kLoop, calls=%fused_computation.72 | loop fusion | flops 13630976 | bytes 10487808 | tf_op jit(solution)/shard_map/reduce_sum | solution.py:44
  66.0 10.3 %all-reduce.4 = (f32[5,64]{1,0:T(8,128)S(1)}, f32[3,64]{1,0:T(4,128)S(1)}) all-reduce(f32[5,64]{1,0:T(8,128)S(1)} %stack.59, f32[3,64]{1,0:T(4,128)S(1)} %pad_maximum_fusion.6), channel_id=1, replica_groups=mesh['shift'=8,'dom'=4] {'dom'}, use_global_device_ids=true, to_apply=%region_5.6 | all-reduce | flops 512 | bytes 4096 | tf_op jit(solution)/shard_map/psum | solution.py:123
  76.3 4.9 %multiply_subtract_fusion.1 = f32[8,64,1024]{2,1,0:T(8,128)} fusion(f32[8,64,1024]{2,1,0:T(8,128)S(1)} %copy-done.2, f32[2,10,64,1024]{3,2,1,0:T(8,128)} %copy-done, f32[]{:T(128)S(6)} %div.77, f32[8,1024]{1,0:T(8,128)S(1)} %get-tuple-element.38, f32[64]{0:T(128)S(1)} %fusion.65, f32[8,1024]{1,0:T(8,128)S(1)} %get-tuple-element.39, ...), kind=kLoop, calls=%fused_computation.70 | loop fusion | flops 9961472 | bytes 8455176 | tf_op jit(solution)/shard_map/sub | solution.py:164
  81.3 60.2 %all-reduce.7.cloned.1.call-done = f32[8,64,1024]{2,1,0:T(8,128)} async-done(((f32[8,64,1024]{2,1,0:T(8,128)}), f32[8,64,1024]{2,1,0:T(8,128)}) %all-reduce.7.cloned.1.call-update) | async-done | bytes 2097168 | tf_op jit(solution)/shard_map/psum | solution.py:166
  141.5 1.2 fusion.78
  142.7 1.3 collective-permute-start.2
  144.0 4.6 %collective-permute-start.3 = (f32[1,64,1024]{2,1,0:T(8,128)S(1)}, f32[1,64,1024]{2,1,0:T(8,128)S(1)}, u32[]{:S(2)}, u32[]{:S(2)}) collective-permute-start(f32[1,64,1024]{2,1,0:T(8,128)S(1)} %get-tuple-element.33), channel_id=1, source_target_pairs={{0,1},{1,2},{2,3},{4,5},{5,6},{6,7},{8,9},{9,10},{10,11},{12,13},{... | collective-permute-start | bytes 786440 | tf_op jit(solution)/shard_map/ppermute | solution.py:22
  148.6 4.0 %fusion.41 = f32[64,64]{1,0:T(8,128)S(1)} fusion(f32[8,64,1024]{2,1,0:T(8,128)} %all-reduce.7.cloned.1.call-done), kind=kOutput, calls=%fused_computation.81 | convolution fusion | flops 402657280 | bytes 2113536 | tf_op jit(solution)/shard_map/znc,zmc->nm/dot_general | solution.py:170
  152.7 3.8 %fusion.42 = f32[64,64]{1,0:T(8,128)S(1)} fusion(f32[8,64,1024]{2,1,0:T(8,128)S(1)} %copy-done.1, f32[1,64,1024]{2,1,0:T(8,128)S(1)} %collective-permute-done.3, f32[1,64,1024]{2,1,0:T(8,128)S(1)} %collective-permute-done.2, f32[1024]{0:T(1024)S(1)} %get-tuple-element.45, f32[1024]{0:T(1024)S(1)} %get-tuple-element.44, f32[8,1024]{1,0:T(8,128)S(1)} %copy-done.5), kind=kOutput, calls=%fused_computation.82 | convolution fusion | flops 408424448 | bytes 4775936 | tf_op jit(solution)/shard_map/znc,zmc->nm/dot_general | solution.py:169
  156.5 21.2 %all-reduce.3 = (f32[64,64]{1,0:T(8,128)}, f32[64,64]{1,0:T(8,128)}) all-reduce(f32[64,64]{1,0:T(8,128)S(1)} %fusion.42, f32[64,64]{1,0:T(8,128)S(1)} %fusion.41), channel_id=1, replica_groups=mesh['shift'=8,'dom'=4] {'dom'}, use_global_device_ids=true, to_apply=%region_11.12 | all-reduce | flops 8192 | bytes 65536 | tf_op jit(solution)/shard_map/psum | solution.py:171
  177.7 1.3 copy.40
  (37 shorter events, 0.8 us)
Async XLA Ops:
  7.2 1.8 copy-start.4
  7.2 134.3 %all-reduce.7.cloned.1.call-start = ((), (), s32[]{:S(2)}) async-start(), calls=%async_computation | async-start | bytes 4194304 | tf_op jit(solution)/shard_map/psum | solution.py:166
  9.7 16.3 %collective-permute-start = (f32[2,65,1024]{2,0,1:T(2,128)S(1)}, f32[2,65,1024]{2,0,1:T(2,128)S(1)}, u32[]{:S(2)}, u32[]{:S(2)}) collective-permute-start(f32[2,65,1024]{2,0,1:T(2,128)S(1)} %copy.8), channel_id=1, source_target_pairs={{0,1},{1,2},{2,3},{4,5},{5,6},{6,7},{8,9},{9,10},{10,11},{12,13},{... | collective-permute-start | bytes 1597448 | tf_op jit(solution)/shard_map/ppermute | solution.py:22
  15.9 15.8 %collective-permute-start.1 = (f32[2,65,1024]{2,0,1:T(2,128)}, f32[2,65,1024]{2,0,1:T(2,128)}, u32[]{:S(2)}, u32[]{:S(2)}) collective-permute-start(f32[2,65,1024]{2,0,1:T(2,128)} %copy.9), channel_id=1, source_target_pairs={{1,0},{2,1},{3,2},{5,4},{6,5},{7,6},{9,8},{10,9},{11,10},{13,12},{... | collective-permute-start | bytes 1597448 | tf_op jit(solution)/shard_map/ppermute | solution.py:23
  33.0 0.7 copy-start.3
  50.8 3.9 %slice-start = ((f32[12,1,1024]{2,1,0:T(1,128)}), f32[10,1,1024]{2,1,0:T(1,128)S(1)}, s32[]{:S(2)}) async-start(f32[12,1,1024]{2,1,0:T(1,128)} %copy-done.3), calls=%async_computation.1 | async-start | bytes 81920 | tf_op jit(solution)/shard_map/slice | solution.py:110
  55.6 8.2 %copy-start = (f32[2,10,64,1024]{3,2,1,0:T(8,128)}, f32[2,10,64,1024]{3,2,1,0:T(8,128)S(1)}, u32[]{:S(2)}) copy-start(f32[2,10,64,1024]{3,2,1,0:T(8,128)S(1)} %maximum_multiply_fusion) | copy-start | bytes 15728644
  62.3 1.6 copy-start.2
  81.2 71.4 %copy-start.5 = (f32[8,1024]{1,0:T(8,128)S(1)}, f32[8,1024]{1,0:T(8,128)}, u32[]{:S(2)}) copy-start(f32[8,1024]{1,0:T(8,128)} %get-tuple-element.37) | copy-start | bytes 98308
  141.5 11.2 %copy-start.1 = (f32[8,64,1024]{2,1,0:T(8,128)S(1)}, f32[8,64,1024]{2,1,0:T(8,128)}, u32[]{:S(2)}) copy-start(f32[8,64,1024]{2,1,0:T(8,128)} %all-reduce.7.cloned.1.call-done) | copy-start | bytes 6291460
  142.7 9.9 %collective-permute-start.2 = (f32[1,64,1024]{2,1,0:T(8,128)S(1)}, f32[1,64,1024]{2,1,0:T(8,128)S(1)}, u32[]{:S(2)}, u32[]{:S(2)}) collective-permute-start(f32[1,64,1024]{2,1,0:T(8,128)S(1)} %get-tuple-element.32), channel_id=1, source_target_pairs={{1,0},{2,1},{3,2},{5,4},{6,5},{7,6},{9,8},{10,9},{11,10},{13,12},{... | collective-permute-start | bytes 786440 | tf_op jit(solution)/shard_map/ppermute | solution.py:23
  144.0 8.7 %collective-permute-start.3 = (f32[1,64,1024]{2,1,0:T(8,128)S(1)}, f32[1,64,1024]{2,1,0:T(8,128)S(1)}, u32[]{:S(2)}, u32[]{:S(2)}) collective-permute-start(f32[1,64,1024]{2,1,0:T(8,128)S(1)} %get-tuple-element.33), channel_id=1, source_target_pairs={{0,1},{1,2},{2,3},{4,5},{5,6},{6,7},{8,9},{9,10},{10,11},{12,13},{... | collective-permute-start | bytes 786440 | tf_op jit(solution)/shard_map/ppermute | solution.py:22
Sparse Core Ops, SparseCore 0:
  81.4 60.0 all-reduce.6
where the time goes:
time: 186 us
  waiting for transfers between devices  73.8 us (40%)
  other arithmetic  38.1 us (20%)
  blocking collectives  31.5 us (17%)
  between operations  14.5 us (8%)
  starting transfers between devices  12.2 us (7%)
  local copies, waits for them, and re-layouts  7.97 us (4%)
  matrix products  7.85 us (4%)
    psum x1, waiting for transfers between devices, on_device(): subspace = lax.psum(weighted, 'shift')  60.2 us
    psum x1, blocking collectives, on_device(): reduced_h, reduced_b = lax.psum((part_h, part_b), 'dom')  21.2 us
    sub x2, other arithmetic, shrink_operate(): return combine(inner, onsite_inner * inner - beside)  18.2 us
    psum x1, blocking collectives, on_device(): second_tot = lax.psum(second_set, 'dom')  10.3 us
    ppermute x2, starting transfers between devices, extended_2(): before = lax.ppermute(last, axis, up)  9.55 us
    ppermute x2, waiting for transfers between devices, extended_2(): before = lax.ppermute(last, axis, up)  8.03 us
    ppermute x2, waiting for transfers between devices, extended_2(): after = lax.ppermute(first, axis, down)  5.49 us
    sub x2, other arithmetic, combine(): shift_re * vector[0] - shift_im * vector[1] - hamil[0]  5.3 us
  transfers between devices with their start and end apart: 5, of which 3 were waited for; matrix products, arithmetic and copies ran while one was open for 3% of the time, Pallas kernels for 0%

commit v1 on v0

v1 whole, which is shorter than its diff:
```python
import functools
import math

import jax
import jax.numpy as jnp
from jax import lax
from jax.experimental import pallas as pl
from jax.experimental.pallas import tpu as pltpu
from jax.sharding import PartitionSpec as P

NX = 32
NY = 32
LANES = 128


CENTRE = 3.0
RADIUS = 2.0
RIDGE = 0.01
PRODUCTS = 8


def lane_iota(rows):
    return lax.broadcasted_iota(jnp.int32, (rows, LANES), 1)


def split(ref_row):
    return [ref_row[:, j * LANES : (j + 1) * LANES] for j in range(ref_row.shape[-1] // LANES)]


def strided_order(parts):
    count = len(parts)
    blocks = LANES // NY
    lane_block = lane_iota(parts[0].shape[0]) // NY
    out = []
    for j in range(count):
        total = None
        for b in range(blocks):
            x = b * count + j
            turn = (NY * (b - x % blocks)) % LANES
            piece = parts[x // blocks]
            piece = pltpu.roll(piece, turn, 1) if turn else piece
            total = piece if total is None else jnp.where(lane_block == b, piece, total)
        out.append(total)
    return out


def natural_order(parts):
    count = len(parts)
    blocks = LANES // NY
    lane_block = lane_iota(parts[0].shape[0]) // NY
    out = []
    for v in range(count):
        total = None
        for c in range(blocks):
            x = v * blocks + c
            turn = (NY * (c - x // count)) % LANES
            piece = parts[x % count]
            piece = pltpu.roll(piece, turn, 1) if turn else piece
            total = piece if total is None else jnp.where(lane_block == c, piece, total)
        out.append(total)
    return out


def plane_neighbours(parts):
    count = len(parts)
    lane = lane_iota(parts[0].shape[0])
    has_low = (lane % NY != 0).astype(jnp.float32)
    has_high = (lane % NY != NY - 1).astype(jnp.float32)
    first = jnp.where(lane < NY, 0.0, pltpu.roll(parts[-1], NY, 1))
    last = jnp.where(lane >= LANES - NY, 0.0, pltpu.roll(parts[0], LANES - NY, 1))
    padded = [first] + parts + [last]
    return [
        padded[j] + padded[j + 2]
        + pltpu.roll(parts[j], 1, 1) * has_low
        + pltpu.roll(parts[j], LANES - 1, 1) * has_high
        for j in range(count)
    ]


def inverses(onsite, shift_re, shift_im):
    diag_re = shift_re - onsite
    scaled = 1.0 / (diag_re * diag_re + shift_im * shift_im)
    return diag_re * scaled, -shift_im * scaled


def krylov_kernel(where, nodes_ref, own, pot, low, high, blocks, b_ref, wide, sums, u, v, inv, onsite):
    k = pl.program_id(0)
    count = pl.num_programs(0)
    planes, cols, cells = own.shape
    vecs = cells // LANES

    @pl.when(k == 0)
    def _():
        sums[...] = jnp.zeros_like(sums)

        def put(z, parts):
            for j, part in enumerate(strided_order(parts)):
                b_ref[z, :, j * LANES : (j + 1) * LANES] = part

        for i in range(2):
            put(i, split(low[i * cols : (i + 1) * cols, :]))
            put(planes + 2 + i, split(high[i * cols : (i + 1) * cols, :]))

        @pl.loop(0, planes)
        def _(z):
            put(z + 2, split(own[z]))

        for start, rows in ((0, low[2 * cols :, :]), (2, pot[...]), (planes + 2, high[2 * cols :, :])):
            for j, part in enumerate(strided_order(split(rows))):
                onsite[start : start + rows.shape[0], j * LANES : (j + 1) * LANES] = 6.0 + part
        for z in range(planes + 4):
            wide[z] = jnp.broadcast_to(onsite[z : z + 1, :], (cols, cells))

    inv_re, inv_im = inverses(onsite[...], nodes_ref[k, 0], nodes_ref[k, 1])
    for z in range(planes + 4):
        inv[0, z] = jnp.broadcast_to(inv_re[z : z + 1], (cols, cells))
        inv[1, z] = jnp.broadcast_to(inv_im[z : z + 1], (cols, cells))

    def at(j):
        return slice(j * LANES, (j + 1) * LANES)

    def factor(c, z, j):
        return inv[c, z, :, at(j)]

    @pl.loop(0, planes + 4)
    def _(z):
        for j in range(vecs):
            value = b_ref[z, :, at(j)]
            u[0, z, :, at(j)] = value * factor(0, z, j)
            u[1, z, :, at(j)] = value * factor(1, z, j)

    def image(field, c, z):
        beside = plane_neighbours([field[c, z, :, at(j)] for j in range(vecs)])
        return [beside[j] + (field[c, z - 1, :, at(j)] + field[c, z + 1, :, at(j)]) for j in range(vecs)]

    @pl.loop(0, planes + 2)
    def _(z):
        low_in = where[1].astype(jnp.float32)
        high_in = where[2].astype(jnp.float32)
        inside = jnp.where(z == 0, low_in, jnp.where(z == planes + 1, high_in, 1.0))
        real = image(u, 0, z + 1)
        imag = image(u, 1, z + 1)
        for j in range(vecs):
            re = (b_ref[z + 1, :, at(j)] + real[j]) * inside
            im = imag[j] * inside
            f_re = factor(0, z + 1, j)
            f_im = factor(1, z + 1, j)
            blocks[0, 0, z, :, at(j)] = re
            blocks[0, 1, z, :, at(j)] = im
            v[0, z, :, at(j)] = re * f_re - im * f_im
            v[1, z, :, at(j)] = re * f_im + im * f_re

    def accumulate(z, acc):
        real = image(v, 0, z + 1)
        imag = image(v, 1, z + 1)
        acc = list(acc)
        for j in range(vecs):
            re = blocks[0, 0, z + 1, :, at(j)]
            im = blocks[0, 1, z + 1, :, at(j)]
            two_re = re + real[j]
            two_im = im + imag[j]
            b = b_ref[z + 2, :, at(j)]
            acc[0] = acc[0] + (re * re + im * im)
            acc[1] = acc[1] + re * b
            acc[2] = acc[2] - im * b
            acc[3] = acc[3] + (re * two_re + im * two_im)
            acc[4] = acc[4] + (re * two_im - im * two_re)
            acc[5] = acc[5] + (two_re * two_re + two_im * two_im)
            acc[6] = acc[6] + two_re * b
            acc[7] = acc[7] - two_im * b
        return tuple(acc)

    zero = jnp.zeros((cols, LANES), jnp.float32)
    acc = lax.fori_loop(0, planes, accumulate, (zero,) * PRODUCTS)
    lane = lane_iota(cols)
    total = sums[...]
    for i in range(PRODUCTS):
        total = jnp.where(lane == i * count + k, jnp.sum(acc[i], axis=1, keepdims=True), total)
    sums[...] = total


def moment_kernel(shifts, weights, blocks, b_ref, onsite, sums, out, coef):
    z = pl.program_id(0)
    nodes = blocks.shape[0]
    cols, cells = b_ref.shape[1:]
    vecs = cells // LANES

    @pl.when(z == 0)
    def _():
        total = sums[...]

        def of(i):
            return pltpu.roll(total, (LANES - i * nodes) % LANES, 1) if i else total

        g_one, q_one_re, q_one_im, g_mix_re, g_mix_im, g_two, q_two_re, q_two_im = map(of, range(PRODUCTS))
        ridge = RIDGE * (g_one + g_two) / 2.0
        determ = (g_one + ridge) * (g_two + ridge) - (g_mix_re * g_mix_re + g_mix_im * g_mix_im)
        one_re = ((g_two + ridge) * q_one_re - (g_mix_re * q_two_re - g_mix_im * q_two_im)) / determ
        one_im = ((g_two + ridge) * q_one_im - (g_mix_re * q_two_im + g_mix_im * q_two_re)) / determ
        two_re = ((g_one + ridge) * q_two_re - (g_mix_re * q_one_re + g_mix_im * q_one_im)) / determ
        two_im = ((g_one + ridge) * q_two_im - (g_mix_re * q_one_im - g_mix_im * q_one_re)) / determ
        w_re = weights[0:1, :]
        w_im = weights[1:2, :]
        scaled = (
            w_re * one_re - w_im * one_im,
            w_re * one_im + w_im * one_re,
            w_re * two_re - w_im * two_im,
            w_re * two_im + w_im * two_re,
        )
        for k in range(nodes):
            for i in range(4):
                coef[k, i] = jnp.broadcast_to(scaled[i][:, k : k + 1], (cols, LANES))

    result = []
    for j in range(vecs):
        at = slice(j * LANES, (j + 1) * LANES)
        b = b_ref[z + 2, :, at]
        total = jnp.zeros((cols, LANES), jnp.float32)
        inv_re, inv_im = inverses(onsite[z + 2, 0:1, at], shifts[0], shifts[1])
        for k in range(nodes):
            re = blocks[k, 0, 0, :, at]
            im = blocks[k, 1, 0, :, at]
            f_re = jnp.broadcast_to(inv_re[k : k + 1], (cols, LANES))
            f_im = jnp.broadcast_to(inv_im[k : k + 1], (cols, LANES))
            y_re = coef[k, 0] * b + coef[k, 2] * re - coef[k, 3] * im
            y_im = coef[k, 1] * b + coef[k, 3] * re + coef[k, 2] * im
            total = total + (f_re * y_re - f_im * y_im)
        result.append(total)
    for j, part in enumerate(natural_order(result)):
        out[0, :, j * LANES : (j + 1) * LANES] = part


def halves(x):
    high = x.astype(jnp.bfloat16)
    return high, (x - high.astype(jnp.float32)).astype(jnp.bfloat16)


def gram_kernel(where, pot, *refs, layout, scale):
    pieces, out, gram, edge = refs[: len(layout)], refs[-3], refs[-2], refs[-1]
    planes, width, cells = out.shape
    for ref, (mask, first) in zip(pieces, layout):
        cols = ref.shape[1]
        start = 0 if cols == width else pl.multiple_of((where[0] ^ mask) * cols, cols)
        for z in range(ref.shape[0]):
            if first + z < planes:
                out[first + z, pl.ds(start, cols), :] = ref[z]
            else:
                edge[pl.ds(start, cols), :] = ref[z]
    cell = lax.broadcasted_iota(jnp.int32, (1, cells), 1)
    x_ok = (cell < cells - NY).astype(jnp.float32)
    y_ok = (cell % NY != NY - 1).astype(jnp.float32)
    total = jnp.zeros((2 * width, 4 * width), jnp.float32)
    for z in range(planes):
        s = out[z]
        after = out[z + 1] if z + 1 < planes else edge[...]
        beside = pltpu.roll(s, cells - NY, 1) * x_ok + pltpu.roll(s, cells - 1, 1) * y_ok + after
        applied = (3.0 + 0.5 * pot[z : z + 1, :]) * s - beside
        s_high, s_low = halves(s)
        a_high, a_low = halves(applied)
        left = jnp.concatenate([s_high, s_low], axis=0)
        right = jnp.concatenate([a_high, s_high, a_low, s_low], axis=0)
        total = total + lax.dot_general(
            left, right, (((1,), (1,)), ((), ())), preferred_element_type=jnp.float32
        )
    both = total[:width, : 2 * width] + total[:width, 2 * width :] + total[width:, : 2 * width]
    gram[...] = both * scale


def butterfly(x, axis):
    count = lax.axis_size(axis)
    step = 1
    while step < count:
        x = x + lax.ppermute(x, axis, [(i, i ^ step) for i in range(count)])
        step *= 2
    return x


def swap(x, mask):
    count = lax.axis_size("shift")
    return lax.ppermute(x, "shift", [(i, i ^ mask) for i in range(count)])


def spread(x):
    count = lax.axis_size("shift")
    if x.shape[1] % 8:
        whole = lax.all_gather(x, "shift", axis=1)
        return [(0, 0, whole.reshape(x.shape[0], -1, x.shape[2]))]
    if count != 8:
        return [(0, 0, x)] + [(m, 0, swap(x, m)) for m in range(1, count)]
    half = x.shape[0] // 2
    a = swap(x, 2)
    b = swap(x, 4)
    d_first = swap(a[:half], 4)
    d_last = swap(b[half:], 2)
    held = [(0, 0, x), (2, 0, a), (4, 0, b), (6, 0, d_first), (6, half, d_last)]
    return held + [(m ^ 1, first, swap(piece, 1)) for m, first, piece in held]


def on_device(samples, potential):
    nodes = lax.axis_size("shift")
    slabs = lax.axis_size("dom")
    planes, width, cells = samples.shape
    cols = width // nodes
    me = lax.axis_index("shift")
    slab = lax.axis_index("dom")
    angles = [math.pi * (k + 0.5) / nodes for k in range(nodes)]
    table = jnp.array(
        [[CENTRE + RADIUS * math.cos(a), RADIUS * math.sin(a)] for a in angles], jnp.float32
    )
    shifts = jnp.broadcast_to(table.T[:, :, None], (2, nodes, LANES))
    spare = [0.0] * (LANES - nodes)
    weights = jnp.array(
        [
            [RADIUS * math.cos(a) / nodes for a in angles] + spare,
            [RADIUS * math.sin(a) / nodes for a in angles] + spare,
        ],
        jnp.float32,
    )
    where = jnp.stack([me, slab > 0, slab < slabs - 1]).astype(jnp.int32)

    def edge(start):
        part = lax.dynamic_slice(samples, (start, me * cols, 0), (2, cols, cells))
        return jnp.concatenate([part.reshape(2 * cols, cells), potential[start : start + 2]], axis=0)

    up = [(i, i + 1) for i in range(slabs - 1)]
    down = [(j, i) for i, j in up]
    low = lax.ppermute(edge(planes - 2), "dom", up)
    high = lax.ppermute(edge(0), "dom", down)

    f32 = jnp.float32
    smem = pl.BlockSpec(memory_space=pltpu.SMEM)

    def full(shape):
        return pl.BlockSpec(shape, lambda *_: (0,) * len(shape))

    if cols % 8:
        source = lax.dynamic_slice_in_dim(samples, me * cols, cols, 1)
        own_spec = full(source.shape)
    else:
        source = samples
        own_spec = pl.BlockSpec((planes, cols, cells), lambda k, w: (0, w[0], 0))
    blocks, b_ext, onsite, sums = pl.pallas_call(
        krylov_kernel,
        grid_spec=pltpu.PrefetchScalarGridSpec(
            num_scalar_prefetch=1,
            grid=(nodes,),
            in_specs=[
                smem,
                own_spec,
                full(potential.shape),
                full(low.shape),
                full(high.shape),
            ],
            out_specs=[
                pl.BlockSpec((1, 2, planes + 2, cols, cells), lambda k, w: (k, 0, 0, 0, 0)),
                full((planes + 4, cols, cells)),
                full((planes + 4, cols, cells)),
                full((cols, LANES)),
            ],
            scratch_shapes=[
                pltpu.VMEM((2, planes + 4, cols, cells), f32),
                pltpu.VMEM((2, planes + 2, cols, cells), f32),
                pltpu.VMEM((2, planes + 4, cols, cells), f32),
                pltpu.VMEM((planes + 4, cells), f32),
            ],
        ),
        out_shape=[
            jax.ShapeDtypeStruct((nodes, 2, planes + 2, cols, cells), f32),
            jax.ShapeDtypeStruct((planes + 4, cols, cells), f32),
            jax.ShapeDtypeStruct((planes + 4, cols, cells), f32),
            jax.ShapeDtypeStruct((cols, LANES), f32),
        ],
        name="krylov",
    )(where, table, source, potential, low, high)

    totals = butterfly(sums, "dom")

    own = pl.pallas_call(
        moment_kernel,
        grid=(planes + 1,),
        in_specs=[
            full(shifts.shape),
            full(weights.shape),
            pl.BlockSpec((nodes, 2, 1, cols, cells), lambda z: (0, 0, z + 1, 0, 0)),
            full(b_ext.shape),
            full(onsite.shape),
            full(totals.shape),
        ],
        out_specs=pl.BlockSpec((1, cols, cells), lambda z: (z, 0, 0)),
        out_shape=jax.ShapeDtypeStruct((planes + 1, cols, cells), f32),
        scratch_shapes=[
            pltpu.VMEM((nodes, 4, cols, LANES), f32),
        ],
        name="moment",
    )(shifts, weights, blocks, b_ext, onsite, totals)

    held = spread(own)
    layout = tuple((mask, first) for mask, first, _ in held)
    vmem = pl.BlockSpec(memory_space=pltpu.VMEM)
    scale = 1.0 / (cells * planes * slabs)
    subspace, gram = pl.pallas_call(
        functools.partial(gram_kernel, layout=layout, scale=scale),
        in_specs=[smem] + [vmem] * (1 + len(held)),
        out_specs=[vmem, vmem],
        out_shape=[
            jax.ShapeDtypeStruct((planes, width, cells), f32),
            jax.ShapeDtypeStruct((width, 2 * width), f32),
        ],
        scratch_shapes=[pltpu.VMEM((width, cells), f32)],
        name="gram",
    )(where, potential, *[piece for _, _, piece in held])
    gram = butterfly(gram, "dom")
    part_h = gram[:, :width]
    return subspace, part_h + part_h.T, gram[:, width:]


def solution(mesh):
    in_specs = (P("dom", None, None), P("dom", None))
    out_specs = (P("dom", None, None), P(), P())
    return jax.shard_map(
        on_device, mesh=mesh, in_specs=in_specs, out_specs=out_specs, check_vma=False
    )
```

time: 186 us -> 88.3 us (0.47)
  waiting for transfers between devices: 73.8 us -> 23.9 us
  other arithmetic: 38.1 us -> 3.39 us
  Pallas kernels: 0 us -> 33.9 us
  blocking collectives: 31.5 us -> 0 us
  between operations: 14.5 us -> 0.79 us
  starting transfers between devices: 12.2 us -> 21 us
  matrix products: 7.85 us -> 0 us
  local copies, waits for them, and re-layouts: 7.97 us -> 4.64 us
    psum x1 -> x0, waiting for transfers between devices: 60.2 us -> none  [on_device(): subspace = lax.psum(weighted, 'shift')]
    pallas_call x0 -> x3, Pallas kernels: none -> 33.9 us  [the longest x1 22.4 us: on_device(): pl.pallas_call(krylov_kernel, grid_spec=pltpu.PrefetchScalarGridSpec(num_...]
    psum x2 -> x0, blocking collectives: 31.5 us -> none  [the longest x1 21.2 us: on_device(): reduced_h, reduced_b = lax.psum((part_h, part_b), 'dom')]
    sub x6 -> x0, other arithmetic: 28.5 us -> none  [the longest x2 18.2 us: shrink_operate(): return combine(inner, onsite_inner * inner - beside)]
    ppermute x4 -> x15, waiting for transfers between devices: 13.5 us -> 23.9 us  [the longest x9 10.4 us: swap(): return lax.ppermute(x, 'shift', [(i, i ^ mask) for i in range(count)])]
    ppermute x4 -> x15, starting transfers between devices: 12.1 us -> 21 us  [the longest x4 8.39 us: butterfly(): x = x + lax.ppermute(x, axis, [(i, i ^ step) for i in range(count)])]
    dot_general x2 -> x0, matrix products: 7.85 us -> none  [the longest x1 4.03 us: on_device(): jnp.einsum('znc,zmc->nm', subspace, subspace, precision=lax.Precision.HIG...]
    another operation x5 -> x1, other arithmetic: 4.3 us -> 0.61 us  [on_device(): where = jnp.stack([me, slab > 0, slab < slabs - 1]).astype(jnp.int32)]
  transfers between devices with their start and end apart: 5 -> 15, of which waited for: 3 -> 11; matrix products, arithmetic and copies ran while one was open for 3% -> 1% of each run, Pallas kernels for 0% -> 0%
where the time goes in v1:
time: 88.3 us; the launch traced here: 87.7 us
  Pallas kernels  33.9 us (38%)
  waiting for transfers between devices  23.9 us (27%)
  starting transfers between devices  21 us (24%)
  local copies, waits for them, and re-layouts  4.64 us (5%)
  other arithmetic  3.39 us (4%)
    pallas_call x1, Pallas kernels, on_device(): pl.pallas_call(krylov_kernel, grid_spec=pltpu.PrefetchScalarGridSpec(num_...  22.4 us
    ppermute x9, waiting for transfers between devices, swap(): return lax.ppermute(x, 'shift', [(i, i ^ mask) for i in range(count)])  10.4 us
    ppermute x4, waiting for transfers between devices, butterfly(): x = x + lax.ppermute(x, axis, [(i, i ^ step) for i in range(count)])  8.93 us
    ppermute x4, starting transfers between devices, butterfly(): x = x + lax.ppermute(x, axis, [(i, i ^ step) for i in range(count)])  8.39 us
    pallas_call x1, Pallas kernels, on_device(): pl.pallas_call(moment_kernel, grid=(planes + 1,), in_specs=[full(shifts.s...  7.6 us
    ppermute x9, starting transfers between devices, swap(): return lax.ppermute(x, 'shift', [(i, i ^ mask) for i in range(count)])  6.38 us
    ppermute x1, starting transfers between devices, on_device(): low = lax.ppermute(edge(planes - 2), 'dom', up)  4.96 us
    ppermute x1, waiting for transfers between devices, on_device(): high = lax.ppermute(edge(0), 'dom', down)  4.34 us
  transfers between devices with their start and end apart: 15, of which 11 were waited for; matrix products, arithmetic and copies ran while one was open for 1% of the time, Pallas kernels for 0%

profile of v1, /device:TPU:0, one launch (start us, length us, event | category | flops | bytes accessed | tf_op | source)
XLA Modules:
  0.0 87.7 jit_solution(5393523806519752867)
XLA Ops:
  0.6 0.8 fusion.1
  1.5 0.9 %dynamic-slice_bitcast_fusion = (f32[16,1024]{1,0:T(8,128)S(1)}, f32[16,1024]{1,0:T(8,128)S(1)}) fusion(f32[8,64,1024]{2,1,0:T(8,128)} %own.1, s32[]{:T(128)S(6)} %select_n.4), kind=kLoop, calls=%fused_computation.2 | loop fusion | bytes 262148 | tf_op jit(solution)/shard_map/reshape | solution.py:323
  2.4 5.0 %collective-permute-start = (f32[18,1024]{1,0:T(8,128)S(1)}, f32[18,1024]{1,0:T(8,128)S(1)}, u32[]{:S(2)}, u32[]{:S(2)}) collective-permute-start(f32[18,1024]{1,0:T(8,128)S(1)} %pad_maximum_fusion), channel_id=1, source_target_pairs={{0,1},{1,2},{2,3},{4,5},{5,6},{6,7},{8,9},{9,10},{10,11},{12,13},{... | collective-permute-start | bytes 221192 | tf_op jit(solution)/shard_map/ppermute | solution.py:327
  7.4 1.3 %collective-permute-start.1 = (f32[18,1024]{1,0:T(8,128)S(1)}, f32[18,1024]{1,0:T(8,128)S(1)}, u32[]{:S(2)}, u32[]{:S(2)}) collective-permute-start(f32[18,1024]{1,0:T(8,128)S(1)} %pad_maximum_fusion.1), channel_id=1, source_target_pairs={{1,0},{2,1},{3,2},{5,4},{6,5},{7,6},{9,8},{10,9},{11,10},{13,12},{... | collective-permute-start | bytes 221192 | tf_op jit(solution)/shard_map/ppermute | solution.py:328
  8.7 0.6 pad_add_fusion.where
  9.6 4.3 %collective-permute-done.1.high = f32[18,1024]{1,0:T(8,128)S(1)} collective-permute-done((f32[18,1024]{1,0:T(8,128)S(1)}, f32[18,1024]{1,0:T(8,128)S(1)}, u32[]{:S(2)}, u32[]{:S(2)}) %collective-permute-start.1) | collective-permute-done | bytes 73760 | tf_op jit(solution)/shard_map/ppermute | solution.py:328
  13.9 0.6 copy-done.10
  14.5 22.4 %krylov.1 = (f32[8,2,10,8,1024]{4,3,2,1,0:T(8,128)}, f32[12,8,1024]{2,1,0:T(8,128)}, f32[12,8,1024]{2,1,0:T(8,128)}, f32[8,128]{1,0:T(8,128)}) custom-call(s32[3]{0:T(128)} %pad_add_fusion.where, f32[8,2]{1,0:T(8,128)} %constant.23.clone.nodes_ref, f32[8,64,1024]{2,1,0:T(8,128)} %own.1, f32[8,1024]{1,0:T(8,128)} %pot.3, f32[18,1024]{1,0:T(8,128)} %copy-done.9, ...), custom_call_target="tpu_custom_call" | custom-call | tf_op jit(solution)/shard_map/krylov/pallas_call | solution.py:342
  36.9 1.6 %collective-permute-start.2 = (f32[8,128]{1,0:T(8,128)}, f32[8,128]{1,0:T(8,128)S(1)}, u32[]{:S(2)}, u32[]{:S(2)}) collective-permute-start(f32[8,128]{1,0:T(8,128)} %get-tuple-element.12), channel_id=1, source_target_pairs={{0,1},{1,0},{2,3},{3,2},{4,5},{5,4},{6,7},{7,6},{8,9},{9,8},{10,11... | collective-permute-start | bytes 12296 | tf_op jit(solution)/shard_map/ppermute | solution.py:273
  38.6 2.2 %collective-permute-done.2 = f32[8,128]{1,0:T(8,128)S(1)} collective-permute-done((f32[8,128]{1,0:T(8,128)}, f32[8,128]{1,0:T(8,128)S(1)}, u32[]{:S(2)}, u32[]{:S(2)}) %collective-permute-start.2) | collective-permute-done | bytes 4128 | tf_op jit(solution)/shard_map/ppermute | solution.py:273
  40.8 0.7 add.20
  41.5 2.6 %collective-permute-start.3 = (f32[8,128]{1,0:T(8,128)S(1)}, f32[8,128]{1,0:T(8,128)S(1)}, u32[]{:S(2)}, u32[]{:S(2)}) collective-permute-start(f32[8,128]{1,0:T(8,128)S(1)} %add.20), channel_id=1, source_target_pairs={{0,2},{1,3},{2,0},{3,1},{4,6},{5,7},{6,4},{7,5},{8,10},{9,11},{10,... | collective-permute-start | bytes 12296 | tf_op jit(solution)/shard_map/ppermute | solution.py:273
  44.1 1.9 %collective-permute-done.3 = f32[8,128]{1,0:T(8,128)S(1)} collective-permute-done((f32[8,128]{1,0:T(8,128)S(1)}, f32[8,128]{1,0:T(8,128)S(1)}, u32[]{:S(2)}, u32[]{:S(2)}) %collective-permute-start.3) | collective-permute-done | bytes 4128 | tf_op jit(solution)/shard_map/ppermute | solution.py:273
  46.0 0.6 add.21.sums
  46.6 0.7 broadcast_in_dim.2.shifts
  47.3 7.6 %moment.1.refs_0_ = f32[9,8,1024]{2,1,0:T(8,128)} custom-call(f32[2,8,128]{2,1,0:T(8,128)} %broadcast_in_dim.2.shifts, f32[2,128]{1,0:T(2,128)} %constant.24.clone.weights, f32[8,2,10,8,1024]{4,3,2,1,0:T(8,128)} %get-tuple-element.9.blocks, f32[12,8,1024]{2,1,0:T(8,128)} %get-tuple-element.10.b_ref, f32[12,8,1024]{2,1,0:T(8,128)} %get-tuple-element.11.onsite, ...), custom_call_target="tpu_custom_call" | custom-call | tf_op jit(solution)/shard_map/moment/pallas_call | solution.py:378
  54.9 1.5 %collective-permute-start.5 = (f32[9,8,1024]{2,1,0:T(8,128)}, f32[9,8,1024]{2,1,0:T(8,128)S(1)}, u32[]{:S(2)}, u32[]{:S(2)}) collective-permute-start(f32[9,8,1024]{2,1,0:T(8,128)} %moment.1.refs_0_), channel_id=1, source_target_pairs={{0,16},{4,20},{8,24},{12,28},{16,0},{20,4},{24,8},{28,12},{1,17},{... | collective-permute-start | bytes 884744 | tf_op jit(solution)/shard_map/ppermute | solution.py:280
  56.4 1.5 %collective-permute-start.4 = (f32[9,8,1024]{2,1,0:T(8,128)}, f32[9,8,1024]{2,1,0:T(8,128)S(1)}, u32[]{:S(2)}, u32[]{:S(2)}) collective-permute-start(f32[9,8,1024]{2,1,0:T(8,128)} %moment.1.refs_0_), channel_id=1, source_target_pairs={{0,8},{4,12},{8,0},{12,4},{16,24},{20,28},{24,16},{28,20},{1,9},{5... | collective-permute-start | bytes 884744 | tf_op jit(solution)/shard_map/ppermute | solution.py:280
  57.9 3.9 %collective-permute-done.5.refs_2_ = f32[9,8,1024]{2,1,0:T(8,128)S(1)} collective-permute-done((f32[9,8,1024]{2,1,0:T(8,128)}, f32[9,8,1024]{2,1,0:T(8,128)S(1)}, u32[]{:S(2)}, u32[]{:S(2)}) %collective-permute-start.5) | collective-permute-done | bytes 294944 | tf_op jit(solution)/shard_map/ppermute | solution.py:280
  61.8 1.6 %collective-permute-start.7 = (f32[5,8,1024]{2,1,0:T(8,128)S(1)}, f32[5,8,1024]{2,1,0:T(8,128)S(1)}, u32[]{:S(2)}, u32[]{:S(2)}) collective-permute-start(f32[5,8,1024]{2,1,0:T(8,128)S(1)} %slice.25), channel_id=1, source_target_pairs={{0,8},{4,12},{8,0},{12,4},{16,24},{20,28},{24,16},{28,20},{1,9},{5... | collective-permute-start | bytes 491528 | tf_op jit(solution)/shard_map/ppermute | solution.py:280
  64.4 1.3 %collective-permute-start.6 = (f32[4,8,1024]{2,1,0:T(8,128)S(1)}, f32[4,8,1024]{2,1,0:T(8,128)S(1)}, u32[]{:S(2)}, u32[]{:S(2)}) collective-permute-start(f32[4,8,1024]{2,1,0:T(8,128)S(1)} %slice.24), channel_id=1, source_target_pairs={{0,16},{4,20},{8,24},{12,28},{16,0},{20,4},{24,8},{28,12},{1,17},{... | collective-permute-start | bytes 393224 | tf_op jit(solution)/shard_map/ppermute | solution.py:280
  65.7 1.5 %collective-permute-done.7.refs_4_ = f32[5,8,1024]{2,1,0:T(8,128)S(1)} collective-permute-done((f32[5,8,1024]{2,1,0:T(8,128)S(1)}, f32[5,8,1024]{2,1,0:T(8,128)S(1)}, u32[]{:S(2)}, u32[]{:S(2)}) %collective-permute-start.7) | collective-permute-done | bytes 163872 | tf_op jit(solution)/shard_map/ppermute | solution.py:280
  67.2 3.1 %collective-permute-done.6.refs_3_ = f32[4,8,1024]{2,1,0:T(8,128)S(1)} collective-permute-done((f32[4,8,1024]{2,1,0:T(8,128)S(1)}, f32[4,8,1024]{2,1,0:T(8,128)S(1)}, u32[]{:S(2)}, u32[]{:S(2)}) %collective-permute-start.6) | collective-permute-done | bytes 131104 | tf_op jit(solution)/shard_map/ppermute | solution.py:280
  70.4 1.3 %collective-permute-done.11.refs_8_ = f32[4,8,1024]{2,1,0:T(8,128)S(1)} collective-permute-done((f32[4,8,1024]{2,1,0:T(8,128)S(1)}, f32[4,8,1024]{2,1,0:T(8,128)S(1)}, u32[]{:S(2)}, u32[]{:S(2)}) %collective-permute-start.11) | collective-permute-done | bytes 131104 | tf_op jit(solution)/shard_map/ppermute | solution.py:280
  72.6 0.7 copy-done.6
  73.3 3.9 %gram.1 = (f32[8,64,1024]{2,1,0:T(8,128)}, f32[64,128]{1,0:T(8,128)}) custom-call(s32[3]{0:T(128)} %pad_add_fusion.where, f32[8,1024]{1,0:T(8,128)} %pot.3, f32[9,8,1024]{2,1,0:T(8,128)} %moment.1.refs_0_, f32[9,8,1024]{2,1,0:T(8,128)} %copy-done.1, f32[9,8,1024]{2,1,0:T(8,128)} %copy-done, f32[4,8,1024]{2,1,0:T(8,128)} %copy-done.7, ...), custom_call_target="tpu_custom_call" | custom-call | tf_op jit(solution)/shard_map/gram/pallas_call | solution.py:401
  77.2 1.6 %collective-permute-start.13 = (f32[64,128]{1,0:T(8,128)}, f32[64,128]{1,0:T(8,128)S(1)}, u32[]{:S(2)}, u32[]{:S(2)}) collective-permute-start(f32[64,128]{1,0:T(8,128)} %get-tuple-element.14), channel_id=1, source_target_pairs={{0,1},{1,0},{2,3},{3,2},{4,5},{5,4},{6,7},{7,6},{8,9},{9,8},{10,11... | collective-permute-start | bytes 98312 | tf_op jit(solution)/shard_map/ppermute | solution.py:273
  78.8 2.5 %collective-permute-done.13 = f32[64,128]{1,0:T(8,128)S(1)} collective-permute-done((f32[64,128]{1,0:T(8,128)}, f32[64,128]{1,0:T(8,128)S(1)}, u32[]{:S(2)}, u32[]{:S(2)}) %collective-permute-start.13) | collective-permute-done | bytes 32800 | tf_op jit(solution)/shard_map/ppermute | solution.py:273
  81.3 0.8 add.22
  82.1 2.6 %collective-permute-start.14 = (f32[64,128]{1,0:T(8,128)S(1)}, f32[64,128]{1,0:T(8,128)S(1)}, u32[]{:S(2)}, u32[]{:S(2)}) collective-permute-start(f32[64,128]{1,0:T(8,128)S(1)} %add.22), channel_id=1, source_target_pairs={{0,2},{1,3},{2,0},{3,1},{4,6},{5,7},{6,4},{7,5},{8,10},{9,11},{10,... | collective-permute-start | bytes 98312 | tf_op jit(solution)/shard_map/ppermute | solution.py:273
  84.7 2.2 %collective-permute-done.14 = f32[64,128]{1,0:T(8,128)S(1)} collective-permute-done((f32[64,128]{1,0:T(8,128)S(1)}, f32[64,128]{1,0:T(8,128)S(1)}, u32[]{:S(2)}, u32[]{:S(2)}) %collective-permute-start.14) | collective-permute-done | bytes 32800 | tf_op jit(solution)/shard_map/ppermute | solution.py:273
  87.0 0.7 fusion
  (39 shorter events, 2.2 us)
Async XLA Ops:
  0.6 46.0 %copy-start.11 = (f32[2,8]{1,0:T(2,128)S(1)}, f32[2,8]{1,0:T(2,128)}, u32[]{:S(2)}) copy-start(f32[2,8]{1,0:T(2,128)} %constant.25) | copy-start | bytes 196
  2.4 7.2 %collective-permute-start = (f32[18,1024]{1,0:T(8,128)S(1)}, f32[18,1024]{1,0:T(8,128)S(1)}, u32[]{:S(2)}, u32[]{:S(2)}) collective-permute-start(f32[18,1024]{1,0:T(8,128)S(1)} %pad_maximum_fusion), channel_id=1, source_target_pairs={{0,1},{1,2},{2,3},{4,5},{5,6},{6,7},{8,9},{9,10},{10,11},{12,13},{... | collective-permute-start | bytes 221192 | tf_op jit(solution)/shard_map/ppermute | solution.py:327
  7.4 6.5 %collective-permute-start.1 = (f32[18,1024]{1,0:T(8,128)S(1)}, f32[18,1024]{1,0:T(8,128)S(1)}, u32[]{:S(2)}, u32[]{:S(2)}) collective-permute-start(f32[18,1024]{1,0:T(8,128)S(1)} %pad_maximum_fusion.1), channel_id=1, source_target_pairs={{1,0},{2,1},{3,2},{5,4},{6,5},{7,6},{9,8},{10,9},{11,10},{13,12},{... | collective-permute-start | bytes 221192 | tf_op jit(solution)/shard_map/ppermute | solution.py:328
  9.6 4.3 %copy-start.9 = (f32[18,1024]{1,0:T(8,128)}, f32[18,1024]{1,0:T(8,128)S(1)}, u32[]{:S(2)}) copy-start(f32[18,1024]{1,0:T(8,128)S(1)} %collective-permute-done.low) | copy-start | bytes 221188
  13.9 0.6 copy-start.10
  36.9 3.9 %collective-permute-start.2 = (f32[8,128]{1,0:T(8,128)}, f32[8,128]{1,0:T(8,128)S(1)}, u32[]{:S(2)}, u32[]{:S(2)}) collective-permute-start(f32[8,128]{1,0:T(8,128)} %get-tuple-element.12), channel_id=1, source_target_pairs={{0,1},{1,0},{2,3},{3,2},{4,5},{5,4},{6,7},{7,6},{8,9},{9,8},{10,11... | collective-permute-start | bytes 12296 | tf_op jit(solution)/shard_map/ppermute | solution.py:273
  41.5 4.5 %collective-permute-start.3 = (f32[8,128]{1,0:T(8,128)S(1)}, f32[8,128]{1,0:T(8,128)S(1)}, u32[]{:S(2)}, u32[]{:S(2)}) collective-permute-start(f32[8,128]{1,0:T(8,128)S(1)} %add.20), channel_id=1, source_target_pairs={{0,2},{1,3},{2,0},{3,1},{4,6},{5,7},{6,4},{7,5},{8,10},{9,11},{10,... | collective-permute-start | bytes 12296 | tf_op jit(solution)/shard_map/ppermute | solution.py:273
  54.9 6.9 %collective-permute-start.5 = (f32[9,8,1024]{2,1,0:T(8,128)}, f32[9,8,1024]{2,1,0:T(8,128)S(1)}, u32[]{:S(2)}, u32[]{:S(2)}) collective-permute-start(f32[9,8,1024]{2,1,0:T(8,128)} %moment.1.refs_0_), channel_id=1, source_target_pairs={{0,16},{4,20},{8,24},{12,28},{16,0},{20,4},{24,8},{28,12},{1,17},{... | collective-permute-start | bytes 884744 | tf_op jit(solution)/shard_map/ppermute | solution.py:280
  56.4 8.0 %collective-permute-start.4 = (f32[9,8,1024]{2,1,0:T(8,128)}, f32[9,8,1024]{2,1,0:T(8,128)S(1)}, u32[]{:S(2)}, u32[]{:S(2)}) collective-permute-start(f32[9,8,1024]{2,1,0:T(8,128)} %moment.1.refs_0_), channel_id=1, source_target_pairs={{0,8},{4,12},{8,0},{12,4},{16,24},{20,28},{24,16},{28,20},{1,9},{5... | collective-permute-start | bytes 884744 | tf_op jit(solution)/shard_map/ppermute | solution.py:280
  61.8 9.9 %copy-start = (f32[9,8,1024]{2,1,0:T(8,128)}, f32[9,8,1024]{2,1,0:T(8,128)S(1)}, u32[]{:S(2)}) copy-start(f32[9,8,1024]{2,1,0:T(8,128)S(1)} %collective-permute-done.5.refs_2_) | copy-start | bytes 884740
  61.8 5.4 %collective-permute-start.7 = (f32[5,8,1024]{2,1,0:T(8,128)S(1)}, f32[5,8,1024]{2,1,0:T(8,128)S(1)}, u32[]{:S(2)}, u32[]{:S(2)}) collective-permute-start(f32[5,8,1024]{2,1,0:T(8,128)S(1)} %slice.25), channel_id=1, source_target_pairs={{0,8},{4,12},{8,0},{12,4},{16,24},{20,28},{24,16},{28,20},{1,9},{5... | collective-permute-start | bytes 491528 | tf_op jit(solution)/shard_map/ppermute | solution.py:280
  63.4 7.0 %collective-permute-start.8 = (f32[9,8,1024]{2,1,0:T(8,128)}, f32[9,8,1024]{2,1,0:T(8,128)S(1)}, u32[]{:S(2)}, u32[]{:S(2)}) collective-permute-start(f32[9,8,1024]{2,1,0:T(8,128)} %moment.1.refs_0_), channel_id=1, source_target_pairs={{0,4},{4,0},{8,12},{12,8},{16,20},{20,16},{24,28},{28,24},{1,5},{5... | collective-permute-start | bytes 884744 | tf_op jit(solution)/shard_map/ppermute | solution.py:280
  63.4 8.3 %collective-permute-start.10 = (f32[9,8,1024]{2,1,0:T(8,128)S(1)}, f32[9,8,1024]{2,1,0:T(8,128)S(1)}, u32[]{:S(2)}, u32[]{:S(2)}) collective-permute-start(f32[9,8,1024]{2,1,0:T(8,128)S(1)} %collective-permute-done.5.refs_2_), channel_id=1, source_target_pairs={{0,4},{4,0},{8,12},{12,8},{16,20},{20,16},{24,28},{28,24},{1,5},{5... | collective-permute-start | bytes 884744 | tf_op jit(solution)/shard_map/ppermute | solution.py:280
  64.4 7.4 %copy-start.1 = (f32[9,8,1024]{2,1,0:T(8,128)}, f32[9,8,1024]{2,1,0:T(8,128)S(1)}, u32[]{:S(2)}) copy-start(f32[9,8,1024]{2,1,0:T(8,128)S(1)} %collective-permute-done.4.refs_1_) | copy-start | bytes 884740
  64.4 7.4 %collective-permute-start.9 = (f32[9,8,1024]{2,1,0:T(8,128)S(1)}, f32[9,8,1024]{2,1,0:T(8,128)S(1)}, u32[]{:S(2)}, u32[]{:S(2)}) collective-permute-start(f32[9,8,1024]{2,1,0:T(8,128)S(1)} %collective-permute-done.4.refs_1_), channel_id=1, source_target_pairs={{0,4},{4,0},{8,12},{12,8},{16,20},{20,16},{24,28},{28,24},{1,5},{5... | collective-permute-start | bytes 884744 | tf_op jit(solution)/shard_map/ppermute | solution.py:280
  64.4 6.0 %collective-permute-start.6 = (f32[4,8,1024]{2,1,0:T(8,128)S(1)}, f32[4,8,1024]{2,1,0:T(8,128)S(1)}, u32[]{:S(2)}, u32[]{:S(2)}) collective-permute-start(f32[4,8,1024]{2,1,0:T(8,128)S(1)} %slice.24), channel_id=1, source_target_pairs={{0,16},{4,20},{8,24},{12,28},{16,0},{20,4},{24,8},{28,12},{1,17},{... | collective-permute-start | bytes 393224 | tf_op jit(solution)/shard_map/ppermute | solution.py:280
  67.2 4.5 %copy-start.5 = (f32[5,8,1024]{2,1,0:T(8,128)}, f32[5,8,1024]{2,1,0:T(8,128)S(1)}, u32[]{:S(2)}) copy-start(f32[5,8,1024]{2,1,0:T(8,128)S(1)} %collective-permute-done.7.refs_4_) | copy-start | bytes 491524
  67.2 4.5 %collective-permute-start.12 = (f32[5,8,1024]{2,1,0:T(8,128)S(1)}, f32[5,8,1024]{2,1,0:T(8,128)S(1)}, u32[]{:S(2)}, u32[]{:S(2)}) collective-permute-start(f32[5,8,1024]{2,1,0:T(8,128)S(1)} %collective-permute-done.7.refs_4_), channel_id=1, source_target_pairs={{0,4},{4,0},{8,12},{12,8},{16,20},{20,16},{24,28},{28,24},{1,5},{5... | collective-permute-start | bytes 491528 | tf_op jit(solution)/shard_map/ppermute | solution.py:280
  70.4 1.4 %copy-start.7 = (f32[4,8,1024]{2,1,0:T(8,128)}, f32[4,8,1024]{2,1,0:T(8,128)S(1)}, u32[]{:S(2)}) copy-start(f32[4,8,1024]{2,1,0:T(8,128)S(1)} %collective-permute-done.6.refs_3_) | copy-start | bytes 393220
  70.4 1.3 %collective-permute-start.11 = (f32[4,8,1024]{2,1,0:T(8,128)S(1)}, f32[4,8,1024]{2,1,0:T(8,128)S(1)}, u32[]{:S(2)}, u32[]{:S(2)}) collective-permute-start(f32[4,8,1024]{2,1,0:T(8,128)S(1)} %collective-permute-done.6.refs_3_), channel_id=1, source_target_pairs={{0,4},{4,0},{8,12},{12,8},{16,20},{20,16},{24,28},{28,24},{1,5},{5... | collective-permute-start | bytes 393224 | tf_op jit(solution)/shard_map/ppermute | solution.py:280
  70.4 1.4 %copy-start.2 = (f32[9,8,1024]{2,1,0:T(8,128)}, f32[9,8,1024]{2,1,0:T(8,128)S(1)}, u32[]{:S(2)}) copy-start(f32[9,8,1024]{2,1,0:T(8,128)S(1)} %collective-permute-done.8.refs_5_) | copy-start | bytes 884740
  71.7 0.6 copy-start.8
  71.7 0.7 copy-start.3
  71.7 0.9 %copy-start.4 = (f32[9,8,1024]{2,1,0:T(8,128)}, f32[9,8,1024]{2,1,0:T(8,128)S(1)}, u32[]{:S(2)}) copy-start(f32[9,8,1024]{2,1,0:T(8,128)S(1)} %collective-permute-done.9.refs_6_) | copy-start | bytes 884740
  72.6 0.7 copy-start.6
  77.2 4.1 %collective-permute-start.13 = (f32[64,128]{1,0:T(8,128)}, f32[64,128]{1,0:T(8,128)S(1)}, u32[]{:S(2)}, u32[]{:S(2)}) collective-permute-start(f32[64,128]{1,0:T(8,128)} %get-tuple-element.14), channel_id=1, source_target_pairs={{0,1},{1,0},{2,3},{3,2},{4,5},{5,4},{6,7},{7,6},{8,9},{9,8},{10,11... | collective-permute-start | bytes 98312 | tf_op jit(solution)/shard_map/ppermute | solution.py:273
  82.1 4.8 %collective-permute-start.14 = (f32[64,128]{1,0:T(8,128)S(1)}, f32[64,128]{1,0:T(8,128)S(1)}, u32[]{:S(2)}, u32[]{:S(2)}) collective-permute-start(f32[64,128]{1,0:T(8,128)S(1)} %add.22), channel_id=1, source_target_pairs={{0,2},{1,3},{2,0},{3,1},{4,6},{5,7},{6,4},{7,5},{8,10},{9,11},{10,... | collective-permute-start | bytes 98312 | tf_op jit(solution)/shard_map/ppermute | solution.py:273

commit v2 on v1

--- a/solution.py
+++ b/solution.py
@@ -3,6 +3,7 @@
 
 import jax
 import jax.numpy as jnp
+import numpy as np
 from jax import lax
 from jax.experimental import pallas as pl
 from jax.experimental.pallas import tpu as pltpu
@@ -83,7 +84,7 @@
     return diag_re * scaled, -shift_im * scaled
 
 
-def krylov_kernel(where, nodes_ref, own, pot, low, high, blocks, b_ref, wide, sums, u, v, inv, onsite):
+def krylov_kernel(where, nodes_ref, own, pot, paired, other, blocks, b_ref, wide, sums, u, v, inv, onsite):
     k = pl.program_id(0)
     count = pl.num_programs(0)
     planes, cols, cells = own.shape
@@ -97,6 +98,9 @@
             for j, part in enumerate(strided_order(parts)):
                 b_ref[z, :, j * LANES : (j + 1) * LANES] = part
 
+        even = where[3] > 0
+        low = jnp.where(even, other[...], paired[...])
+        high = jnp.where(even, paired[...], other[...])
         for i in range(2):
             put(i, split(low[i * cols : (i + 1) * cols, :]))
             put(planes + 2 + i, split(high[i * cols : (i + 1) * cols, :]))
@@ -122,8 +126,7 @@
     def factor(c, z, j):
         return inv[c, z, :, at(j)]
 
-    @pl.loop(0, planes + 4)
-    def _(z):
+    for z in range(planes + 4):
         for j in range(vecs):
             value = b_ref[z, :, at(j)]
             u[0, z, :, at(j)] = value * factor(0, z, j)
@@ -133,20 +136,21 @@
         beside = plane_neighbours([field[c, z, :, at(j)] for j in range(vecs)])
         return [beside[j] + (field[c, z - 1, :, at(j)] + field[c, z + 1, :, at(j)]) for j in range(vecs)]
 
-    @pl.loop(0, planes + 2)
-    def _(z):
-        low_in = where[1].astype(jnp.float32)
-        high_in = where[2].astype(jnp.float32)
-        inside = jnp.where(z == 0, low_in, jnp.where(z == planes + 1, high_in, 1.0))
+    outside = {0: where[1].astype(jnp.float32), planes + 1: where[2].astype(jnp.float32)}
+    for z in range(planes + 2):
         real = image(u, 0, z + 1)
         imag = image(u, 1, z + 1)
         for j in range(vecs):
-            re = (b_ref[z + 1, :, at(j)] + real[j]) * inside
-            im = imag[j] * inside
+            re = b_ref[z + 1, :, at(j)] + real[j]
+            im = imag[j]
+            if z in outside:
+                re = re * outside[z]
+                im = im * outside[z]
             f_re = factor(0, z + 1, j)
             f_im = factor(1, z + 1, j)
-            blocks[0, 0, z, :, at(j)] = re
-            blocks[0, 1, z, :, at(j)] = im
+            if z > 0:
+                blocks[0, 0, z - 1, :, at(j)] = re
+                blocks[0, 1, z - 1, :, at(j)] = im
             v[0, z, :, at(j)] = re * f_re - im * f_im
             v[1, z, :, at(j)] = re * f_im + im * f_re
 
@@ -155,8 +159,8 @@
         imag = image(v, 1, z + 1)
         acc = list(acc)
         for j in range(vecs):
-            re = blocks[0, 0, z + 1, :, at(j)]
-            im = blocks[0, 1, z + 1, :, at(j)]
+            re = blocks[0, 0, z, :, at(j)]
+            im = blocks[0, 1, z, :, at(j)]
             two_re = re + real[j]
             two_im = im + imag[j]
             b = b_ref[z + 2, :, at(j)]
@@ -171,7 +175,9 @@
         return tuple(acc)
 
     zero = jnp.zeros((cols, LANES), jnp.float32)
-    acc = lax.fori_loop(0, planes, accumulate, (zero,) * PRODUCTS)
+    acc = (zero,) * PRODUCTS
+    for z in range(planes):
+        acc = accumulate(z, acc)
     lane = lane_iota(cols)
     total = sums[...]
     for i in range(PRODUCTS):
@@ -180,12 +186,12 @@
 
 
 def moment_kernel(shifts, weights, blocks, b_ref, onsite, sums, out, coef):
-    z = pl.program_id(0)
+    step = pl.program_id(0)
     nodes = blocks.shape[0]
     cols, cells = b_ref.shape[1:]
     vecs = cells // LANES
 
-    @pl.when(z == 0)
+    @pl.when(step == 0)
     def _():
         total = sums[...]
 
@@ -211,23 +217,25 @@
             for i in range(4):
                 coef[k, i] = jnp.broadcast_to(scaled[i][:, k : k + 1], (cols, LANES))
 
-    result = []
-    for j in range(vecs):
-        at = slice(j * LANES, (j + 1) * LANES)
-        b = b_ref[z + 2, :, at]
-        total = jnp.zeros((cols, LANES), jnp.float32)
-        inv_re, inv_im = inverses(onsite[z + 2, 0:1, at], shifts[0], shifts[1])
-        for k in range(nodes):
-            re = blocks[k, 0, 0, :, at]
-            im = blocks[k, 1, 0, :, at]
-            f_re = jnp.broadcast_to(inv_re[k : k + 1], (cols, LANES))
-            f_im = jnp.broadcast_to(inv_im[k : k + 1], (cols, LANES))
-            y_re = coef[k, 0] * b + coef[k, 2] * re - coef[k, 3] * im
-            y_im = coef[k, 1] * b + coef[k, 3] * re + coef[k, 2] * im
-            total = total + (f_re * y_re - f_im * y_im)
-        result.append(total)
-    for j, part in enumerate(natural_order(result)):
-        out[0, :, j * LANES : (j + 1) * LANES] = part
+    for i in range(out.shape[0]):
+        z = step * out.shape[0] + i
+        result = []
+        for j in range(vecs):
+            at = slice(j * LANES, (j + 1) * LANES)
+            b = b_ref[z + 2, :, at]
+            total = jnp.zeros((cols, LANES), jnp.float32)
+            inv_re, inv_im = inverses(onsite[z + 2, 0:1, at], shifts[0], shifts[1])
+            for k in range(nodes):
+                re = blocks[k, 0, i, :, at]
+                im = blocks[k, 1, i, :, at]
+                f_re = jnp.broadcast_to(inv_re[k : k + 1], (cols, LANES))
+                f_im = jnp.broadcast_to(inv_im[k : k + 1], (cols, LANES))
+                y_re = coef[k, 0] * b + coef[k, 2] * re - coef[k, 3] * im
+                y_im = coef[k, 1] * b + coef[k, 3] * re + coef[k, 2] * im
+                total = total + (f_re * y_re - f_im * y_im)
+            result.append(total)
+        for j, part in enumerate(natural_order(result)):
+            out[i, :, j * LANES : (j + 1) * LANES] = part
 
 
 def halves(x):
@@ -268,6 +276,9 @@
 
 def butterfly(x, axis):
     count = lax.axis_size(axis)
+    if count == 4:
+        far = [lax.ppermute(x, axis, [(i, i ^ m) for i in range(4)]) for m in (2, 3, 1)]
+        return (x + far[2]) + (far[0] + far[1])
     step = 1
     while step < count:
         x = x + lax.ppermute(x, axis, [(i, i ^ step) for i in range(count)])
@@ -304,10 +315,10 @@
     me = lax.axis_index("shift")
     slab = lax.axis_index("dom")
     angles = [math.pi * (k + 0.5) / nodes for k in range(nodes)]
-    table = jnp.array(
-        [[CENTRE + RADIUS * math.cos(a), RADIUS * math.sin(a)] for a in angles], jnp.float32
+    table = np.array(
+        [[CENTRE + RADIUS * math.cos(a), RADIUS * math.sin(a)] for a in angles], np.float32
     )
-    shifts = jnp.broadcast_to(table.T[:, :, None], (2, nodes, LANES))
+    shifts = np.ascontiguousarray(np.broadcast_to(table.T[:, :, None], (2, nodes, LANES)))
     spare = [0.0] * (LANES - nodes)
     weights = jnp.array(
         [
@@ -316,16 +327,20 @@
         ],
         jnp.float32,
     )
-    where = jnp.stack([me, slab > 0, slab < slabs - 1]).astype(jnp.int32)
+    where = jnp.stack([me, slab > 0, slab < slabs - 1, slab % 2 == 0]).astype(jnp.int32)
 
     def edge(start):
         part = lax.dynamic_slice(samples, (start, me * cols, 0), (2, cols, cells))
-        return jnp.concatenate([part.reshape(2 * cols, cells), potential[start : start + 2]], axis=0)
-
-    up = [(i, i + 1) for i in range(slabs - 1)]
-    down = [(j, i) for i, j in up]
-    low = lax.ppermute(edge(planes - 2), "dom", up)
-    high = lax.ppermute(edge(0), "dom", down)
+        rows = lax.dynamic_slice(potential, (start, 0), (2, cells))
+        return jnp.concatenate([part.reshape(2 * cols, cells), rows], axis=0)
+
+    def pairs(start):
+        ups = [(i, i + 1) for i in range(start, slabs - 1, 2)]
+        return ups + [(j, i) for i, j in ups]
+
+    even = slab % 2 == 0
+    paired = lax.ppermute(edge(jnp.where(even, planes - 2, 0)), "dom", pairs(0))
+    other = lax.ppermute(edge(jnp.where(even, 0, planes - 2)), "dom", pairs(1))
 
     f32 = jnp.float32
     smem = pl.BlockSpec(memory_space=pltpu.SMEM)
@@ -348,11 +363,11 @@
                 smem,
                 own_spec,
                 full(potential.shape),
-                full(low.shape),
-                full(high.shape),
+                full(paired.shape),
+                full(other.shape),
             ],
             out_specs=[
-                pl.BlockSpec((1, 2, planes + 2, cols, cells), lambda k, w: (k, 0, 0, 0, 0)),
+                pl.BlockSpec((1, 2, planes + 1, cols, cells), lambda k, w: (k, 0, 0, 0, 0)),
                 full((planes + 4, cols, cells)),
                 full((planes + 4, cols, cells)),
                 full((cols, LANES)),
@@ -365,28 +380,29 @@
             ],
         ),
         out_shape=[
-            jax.ShapeDtypeStruct((nodes, 2, planes + 2, cols, cells), f32),
+            jax.ShapeDtypeStruct((nodes, 2, planes + 1, cols, cells), f32),
             jax.ShapeDtypeStruct((planes + 4, cols, cells), f32),
             jax.ShapeDtypeStruct((planes + 4, cols, cells), f32),
             jax.ShapeDtypeStruct((cols, LANES), f32),
         ],
         name="krylov",
-    )(where, table, source, potential, low, high)
+    )(where, table, source, potential, paired, other)
 
     totals = butterfly(sums, "dom")
 
+    group = 3 if (planes + 1) % 3 == 0 else 1
     own = pl.pallas_call(
         moment_kernel,
-        grid=(planes + 1,),
+        grid=((planes + 1) // group,),
         in_specs=[
             full(shifts.shape),
             full(weights.shape),
-            pl.BlockSpec((nodes, 2, 1, cols, cells), lambda z: (0, 0, z + 1, 0, 0)),
+            pl.BlockSpec((nodes, 2, group, cols, cells), lambda z: (0, 0, z, 0, 0)),
             full(b_ext.shape),
             full(onsite.shape),
             full(totals.shape),
         ],
-        out_specs=pl.BlockSpec((1, cols, cells), lambda z: (z, 0, 0)),
+        out_specs=pl.BlockSpec((group, cols, cells), lambda z: (z, 0, 0)),
         out_shape=jax.ShapeDtypeStruct((planes + 1, cols, cells), f32),
         scratch_shapes=[
             pltpu.VMEM((nodes, 4, cols, LANES), f32),

time: 88.3 us -> 69.3 us (0.78)
  Pallas kernels: 33.9 us -> 19.7 us
  waiting for transfers between devices: 23.9 us -> 20.1 us
  starting transfers between devices: 21 us -> 20.1 us
    pallas_call x1, Pallas kernels: 22.4 us -> 10.8 us  [on_device(): pl.pallas_call(krylov_kernel, grid_spec=pltpu.PrefetchScalarGridSpec(num_...]
    ppermute x6 -> x8, waiting for transfers between devices: 13.5 us -> 8.29 us  [the longest x6 6.81 us: butterfly(): lax.ppermute(x, axis, [(i, i ^ m) for i in range(4)])]
    pallas_call x1, Pallas kernels: 7.6 us -> 5.01 us  [on_device(): pl.pallas_call(moment_kernel, grid=((planes + 1) // group,), in_specs=[fu...]
    ppermute x9, waiting for transfers between devices: 10.4 us -> 11.8 us  [swap(): return lax.ppermute(x, 'shift', [(i, i ^ mask) for i in range(count)])]
    unnamed x24 -> x22, local copies, waits for them, and re-layouts: 2.15 us -> 2.79 us
    ppermute x6 -> x8, starting transfers between devices: 14.6 us -> 14.5 us  [the longest x6 10.7 us: butterfly(): lax.ppermute(x, axis, [(i, i ^ m) for i in range(4)])]
    add x4 -> x2, other arithmetic: 2.06 us -> 2.05 us  [butterfly(): return x + far[2] + (far[0] + far[1])]
  transfers between devices with their start and end apart: 15 -> 17, of which waited for: 11 -> 10; matrix products, arithmetic and copies ran while one was open for 1% -> 1% of each run, Pallas kernels for 0% -> 0%
where the time goes in v2:
time: 69.3 us; the launch traced here: 68.8 us
  starting transfers between devices  20.1 us (29%)
  waiting for transfers between devices  20.1 us (29%)
  Pallas kernels  19.7 us (28%)
  local copies, waits for them, and re-layouts  4.63 us (7%)
  other arithmetic  3.39 us (5%)
  between operations  0.79 us (1%)
    ppermute x9, waiting for transfers between devices, swap(): return lax.ppermute(x, 'shift', [(i, i ^ mask) for i in range(count)])  11.8 us
    pallas_call x1, Pallas kernels, on_device(): pl.pallas_call(krylov_kernel, grid_spec=pltpu.PrefetchScalarGridSpec(num_...  10.8 us
    ppermute x6, starting transfers between devices, butterfly(): lax.ppermute(x, axis, [(i, i ^ m) for i in range(4)])  10.7 us
    ppermute x6, waiting for transfers between devices, butterfly(): lax.ppermute(x, axis, [(i, i ^ m) for i in range(4)])  6.81 us
    ppermute x9, starting transfers between devices, swap(): return lax.ppermute(x, 'shift', [(i, i ^ mask) for i in range(count)])  5.66 us
    pallas_call x1, Pallas kernels, on_device(): pl.pallas_call(moment_kernel, grid=((planes + 1) // group,), in_specs=[fu...  5.01 us
    pallas_call x1, Pallas kernels, on_device(): pl.pallas_call(functools.partial(gram_kernel, layout=layout, scale=scale)...  3.94 us
    ppermute x1, starting transfers between devices, on_device(): paired = lax.ppermute(edge(jnp.where(even, planes - 2, 0)), 'dom', pairs(0))  3.12 us
  transfers between devices with their start and end apart: 17, of which 10 were waited for; matrix products, arithmetic and copies ran while one was open for 1% of the time, Pallas kernels for 0%

profile of v2, /device:TPU:0, one launch (start us, length us, event | category | flops | bytes accessed | tf_op | source)
XLA Modules:
  0.0 68.8 jit_solution(12575342287979337497)
XLA Ops:
  0.7 0.8 %constant_dynamic-slice_fusion = (f32[2,1024]{1,0:T(2,128)S(1)}, f32[2,1024]{1,0:T(2,128)S(1)}) fusion(f32[8,1024]{1,0:T(8,128)} %pot.3, s32[]{:T(128)S(6)} %select_n.27, s32[]{:T(128)S(6)} %select_n.25), kind=kLoop, calls=%fused_computation.7 | loop fusion | bytes 32776 | tf_op jit(solution)/shard_map/dynamic_slice | solution.py:334
  1.5 0.9 %dynamic-slice_bitcast_fusion = (f32[16,1024]{1,0:T(8,128)S(1)}, f32[16,1024]{1,0:T(8,128)S(1)}) fusion(f32[8,64,1024]{2,1,0:T(8,128)} %own.1, s32[]{:T(128)S(6)} %select_n.27, s32[]{:T(128)S(6)} %select_n.26, s32[]{:T(128)S(6)} %select_n.25), kind=kLoop, calls=%fused_computation.2 | loop fusion | bytes 262156 | tf_op jit(solution)/shard_map/reshape | solution.py:335
  2.4 3.1 %collective-permute-start = (f32[18,1024]{1,0:T(8,128)S(1)}, f32[18,1024]{1,0:T(8,128)S(1)}, u32[]{:S(2)}, u32[]{:S(2)}) collective-permute-start(f32[18,1024]{1,0:T(8,128)S(1)} %pad_maximum_fusion), channel_id=1, source_target_pairs={{0,1},{2,3},{1,0},{3,2},{4,5},{6,7},{5,4},{7,6},{8,9},{10,11},{9,8... | collective-permute-start | bytes 221192 | tf_op jit(solution)/shard_map/ppermute | solution.py:342
  5.5 0.7 collective-permute-start.1
  6.2 0.6 pad_add_fusion.where
  6.8 1.5 %collective-permute-done.paired = f32[18,1024]{1,0:T(8,128)S(1)} collective-permute-done((f32[18,1024]{1,0:T(8,128)S(1)}, f32[18,1024]{1,0:T(8,128)S(1)}, u32[]{:S(2)}, u32[]{:S(2)}) %collective-permute-start) | collective-permute-done | bytes 73760 | tf_op jit(solution)/shard_map/ppermute | solution.py:342
  8.3 0.6 copy-done.9
  9.0 0.6 copy-done.10
  9.6 10.8 %krylov.1 = (f32[8,2,9,8,1024]{4,3,2,1,0:T(8,128)}, f32[12,8,1024]{2,1,0:T(8,128)}, f32[12,8,1024]{2,1,0:T(8,128)}, f32[8,128]{1,0:T(8,128)}) custom-call(s32[4]{0:T(128)} %pad_add_fusion.where, f32[8,2]{1,0:T(8,128)} %constant.42.clone.nodes_ref, f32[8,64,1024]{2,1,0:T(8,128)} %own.1, f32[8,1024]{1,0:T(8,128)} %pot.3, f32[18,1024]{1,0:T(8,128)} %copy-done.9, ...), custom_call_target="tpu_custom_call" | custom-call | tf_op jit(solution)/shard_map/krylov/pallas_call | solution.py:357
  20.4 3.9 %collective-permute-start.4 = (f32[8,128]{1,0:T(8,128)}, f32[8,128]{1,0:T(8,128)S(1)}, u32[]{:S(2)}, u32[]{:S(2)}) collective-permute-start(f32[8,128]{1,0:T(8,128)} %get-tuple-element.12), channel_id=1, source_target_pairs={{0,3},{1,2},{2,1},{3,0},{4,7},{5,6},{6,5},{7,4},{8,11},{9,10},{10,... | collective-permute-start | bytes 12296 | tf_op jit(solution)/shard_map/ppermute | solution.py:280
  24.3 1.9 %collective-permute-start.3 = (f32[8,128]{1,0:T(8,128)}, f32[8,128]{1,0:T(8,128)S(1)}, u32[]{:S(2)}, u32[]{:S(2)}) collective-permute-start(f32[8,128]{1,0:T(8,128)} %get-tuple-element.12), channel_id=1, source_target_pairs={{0,2},{1,3},{2,0},{3,1},{4,6},{5,7},{6,4},{7,5},{8,10},{9,11},{10,... | collective-permute-start | bytes 12296 | tf_op jit(solution)/shard_map/ppermute | solution.py:280
  26.7 2.3 %collective-permute-done.3 = f32[8,128]{1,0:T(8,128)S(1)} collective-permute-done((f32[8,128]{1,0:T(8,128)}, f32[8,128]{1,0:T(8,128)S(1)}, u32[]{:S(2)}, u32[]{:S(2)}) %collective-permute-start.3) | collective-permute-done | bytes 4128 | tf_op jit(solution)/shard_map/ppermute | solution.py:280
  29.1 1.0 %collective-permute-done.2 = f32[8,128]{1,0:T(8,128)S(1)} collective-permute-done((f32[8,128]{1,0:T(8,128)}, f32[8,128]{1,0:T(8,128)S(1)}, u32[]{:S(2)}, u32[]{:S(2)}) %collective-permute-start.2) | collective-permute-done | bytes 4128 | tf_op jit(solution)/shard_map/ppermute | solution.py:280
  30.1 1.3 %add_add_fusion.1.sums = f32[8,128]{1,0:T(8,128)} fusion(f32[8,128]{1,0:T(8,128)S(1)} %collective-permute-done.3, f32[8,128]{1,0:T(8,128)S(1)} %collective-permute-done.4, f32[8,128]{1,0:T(8,128)} %get-tuple-element.12, f32[8,128]{1,0:T(8,128)S(1)} %collective-permute-done.2), kind=kLoop, calls=%fused_computation.6 | loop fusion | flops 3072 | bytes 20480 | tf_op jit(solution)/shard_map/add | solution.py:281
  31.3 5.0 %moment.1.refs_0_ = f32[9,8,1024]{2,1,0:T(8,128)} custom-call(f32[2,8,128]{2,1,0:T(8,128)} %constant.43.clone.shifts, f32[2,128]{1,0:T(2,128)} %constant.41.clone.weights, f32[8,2,9,8,1024]{4,3,2,1,0:T(8,128)} %get-tuple-element.9.blocks, f32[12,8,1024]{2,1,0:T(8,128)} %get-tuple-element.10.b_ref, f32[12,8,1024]{2,1,0:T(8,128)} %get-tuple-element.11.onsite, ...), custom_call_target="tpu_custom_call" | custom-call | tf_op jit(solution)/shard_map/moment/pallas_call | solution.py:394
  36.3 1.5 %collective-permute-start.6 = (f32[9,8,1024]{2,1,0:T(8,128)}, f32[9,8,1024]{2,1,0:T(8,128)S(1)}, u32[]{:S(2)}, u32[]{:S(2)}) collective-permute-start(f32[9,8,1024]{2,1,0:T(8,128)} %moment.1.refs_0_), channel_id=1, source_target_pairs={{0,16},{4,20},{8,24},{12,28},{16,0},{20,4},{24,8},{28,12},{1,17},{... | collective-permute-start | bytes 884744 | tf_op jit(solution)/shard_map/ppermute | solution.py:291
  37.9 1.5 %collective-permute-start.5 = (f32[9,8,1024]{2,1,0:T(8,128)}, f32[9,8,1024]{2,1,0:T(8,128)S(1)}, u32[]{:S(2)}, u32[]{:S(2)}) collective-permute-start(f32[9,8,1024]{2,1,0:T(8,128)} %moment.1.refs_0_), channel_id=1, source_target_pairs={{0,8},{4,12},{8,0},{12,4},{16,24},{20,28},{24,16},{28,20},{1,9},{5... | collective-permute-start | bytes 884744 | tf_op jit(solution)/shard_map/ppermute | solution.py:291
  39.4 3.9 %collective-permute-done.6.refs_2_ = f32[9,8,1024]{2,1,0:T(8,128)S(1)} collective-permute-done((f32[9,8,1024]{2,1,0:T(8,128)}, f32[9,8,1024]{2,1,0:T(8,128)S(1)}, u32[]{:S(2)}, u32[]{:S(2)}) %collective-permute-start.6) | collective-permute-done | bytes 294944 | tf_op jit(solution)/shard_map/ppermute | solution.py:291
  43.3 1.6 %collective-permute-start.8 = (f32[5,8,1024]{2,1,0:T(8,128)S(1)}, f32[5,8,1024]{2,1,0:T(8,128)S(1)}, u32[]{:S(2)}, u32[]{:S(2)}) collective-permute-start(f32[5,8,1024]{2,1,0:T(8,128)S(1)} %slice.17), channel_id=1, source_target_pairs={{0,8},{4,12},{8,0},{12,4},{16,24},{20,28},{24,16},{28,20},{1,9},{5... | collective-permute-start | bytes 491528 | tf_op jit(solution)/shard_map/ppermute | solution.py:291
  45.4 1.2 %collective-permute-done.5.refs_1_ = f32[9,8,1024]{2,1,0:T(8,128)S(1)} collective-permute-done((f32[9,8,1024]{2,1,0:T(8,128)}, f32[9,8,1024]{2,1,0:T(8,128)S(1)}, u32[]{:S(2)}, u32[]{:S(2)}) %collective-permute-start.5) | collective-permute-done | bytes 294944 | tf_op jit(solution)/shard_map/ppermute | solution.py:291
  46.6 0.6 collective-permute-start.7
  47.1 1.5 %collective-permute-done.8.refs_4_ = f32[5,8,1024]{2,1,0:T(8,128)S(1)} collective-permute-done((f32[5,8,1024]{2,1,0:T(8,128)S(1)}, f32[5,8,1024]{2,1,0:T(8,128)S(1)}, u32[]{:S(2)}, u32[]{:S(2)}) %collective-permute-start.8) | collective-permute-done | bytes 163872 | tf_op jit(solution)/shard_map/ppermute | solution.py:291
  48.7 3.9 %collective-permute-done.7.refs_3_ = f32[4,8,1024]{2,1,0:T(8,128)S(1)} collective-permute-done((f32[4,8,1024]{2,1,0:T(8,128)S(1)}, f32[4,8,1024]{2,1,0:T(8,128)S(1)}, u32[]{:S(2)}, u32[]{:S(2)}) %collective-permute-start.7) | collective-permute-done | bytes 131104 | tf_op jit(solution)/shard_map/ppermute | solution.py:291
  52.6 1.3 %collective-permute-done.12.refs_8_ = f32[4,8,1024]{2,1,0:T(8,128)S(1)} collective-permute-done((f32[4,8,1024]{2,1,0:T(8,128)S(1)}, f32[4,8,1024]{2,1,0:T(8,128)S(1)}, u32[]{:S(2)}, u32[]{:S(2)}) %collective-permute-start.12) | collective-permute-done | bytes 131104 | tf_op jit(solution)/shard_map/ppermute | solution.py:291
  54.8 0.7 copy-done.6
  55.5 3.9 %gram.1 = (f32[8,64,1024]{2,1,0:T(8,128)}, f32[64,128]{1,0:T(8,128)}) custom-call(s32[4]{0:T(128)} %pad_add_fusion.where, f32[8,1024]{1,0:T(8,128)} %pot.3, f32[9,8,1024]{2,1,0:T(8,128)} %moment.1.refs_0_, f32[9,8,1024]{2,1,0:T(8,128)} %copy-done.1, f32[9,8,1024]{2,1,0:T(8,128)} %copy-done, f32[4,8,1024]{2,1,0:T(8,128)} %copy-done.7, ...), custom_call_target="tpu_custom_call" | custom-call | tf_op jit(solution)/shard_map/gram/pallas_call | solution.py:417
  59.4 2.8 %collective-permute-start.16 = (f32[64,128]{1,0:T(8,128)}, f32[64,128]{1,0:T(8,128)S(1)}, u32[]{:S(2)}, u32[]{:S(2)}) collective-permute-start(f32[64,128]{1,0:T(8,128)} %get-tuple-element.14), channel_id=1, source_target_pairs={{0,3},{1,2},{2,1},{3,0},{4,7},{5,6},{6,5},{7,4},{8,11},{9,10},{10,... | collective-permute-start | bytes 98312 | tf_op jit(solution)/shard_map/ppermute | solution.py:280
  62.2 1.5 %collective-permute-start.14 = (f32[64,128]{1,0:T(8,128)}, f32[64,128]{1,0:T(8,128)S(1)}, u32[]{:S(2)}, u32[]{:S(2)}) collective-permute-start(f32[64,128]{1,0:T(8,128)} %get-tuple-element.14), channel_id=1, source_target_pairs={{0,1},{1,0},{2,3},{3,2},{4,5},{5,4},{6,7},{7,6},{8,9},{9,8},{10,11... | collective-permute-start | bytes 98312 | tf_op jit(solution)/shard_map/ppermute | solution.py:280
  63.8 1.6 %collective-permute-done.16 = f32[64,128]{1,0:T(8,128)S(1)} collective-permute-done((f32[64,128]{1,0:T(8,128)}, f32[64,128]{1,0:T(8,128)S(1)}, u32[]{:S(2)}, u32[]{:S(2)}) %collective-permute-start.16) | collective-permute-done | bytes 32800 | tf_op jit(solution)/shard_map/ppermute | solution.py:280
  65.4 1.8 %collective-permute-done.15 = f32[64,128]{1,0:T(8,128)S(1)} collective-permute-done((f32[64,128]{1,0:T(8,128)}, f32[64,128]{1,0:T(8,128)S(1)}, u32[]{:S(2)}, u32[]{:S(2)}) %collective-permute-start.15) | collective-permute-done | bytes 32800 | tf_op jit(solution)/shard_map/ppermute | solution.py:280
  67.3 0.8 %add_add_fusion = f32[64,128]{1,0:T(8,128)S(1)} fusion(f32[64,128]{1,0:T(8,128)S(1)} %collective-permute-done.15, f32[64,128]{1,0:T(8,128)S(1)} %collective-permute-done.16, f32[64,128]{1,0:T(8,128)} %get-tuple-element.14, f32[64,128]{1,0:T(8,128)S(1)} %collective-permute-done.14), kind=kLoop, calls=%fused_computation.5 | loop fusion | flops 24576 | bytes 163840 | tf_op jit(solution)/shard_map/add | solution.py:281
  68.1 0.7 %fusion = (f32[64,64]{1,0:T(8,128)}, f32[64,64]{1,0:T(8,128)}) fusion(f32[64,128]{1,0:T(8,128)S(1)} %add_add_fusion, f32[64,64]{0,1:T(8,128)S(1)} %copy.8), kind=kLoop, calls=%fused_computation.10 | loop fusion | flops 4096 | bytes 81920 | tf_op jit(solution)/shard_map/slice | solution.py:430
  (38 shorter events, 2.0 us)
Async XLA Ops:
  2.4 5.9 %collective-permute-start = (f32[18,1024]{1,0:T(8,128)S(1)}, f32[18,1024]{1,0:T(8,128)S(1)}, u32[]{:S(2)}, u32[]{:S(2)}) collective-permute-start(f32[18,1024]{1,0:T(8,128)S(1)} %pad_maximum_fusion), channel_id=1, source_target_pairs={{0,1},{2,3},{1,0},{3,2},{4,5},{6,7},{5,4},{7,6},{8,9},{10,11},{9,8... | collective-permute-start | bytes 221192 | tf_op jit(solution)/shard_map/ppermute | solution.py:342
  5.5 2.8 %collective-permute-start.1 = (f32[18,1024]{1,0:T(8,128)S(1)}, f32[18,1024]{1,0:T(8,128)S(1)}, u32[]{:S(2)}, u32[]{:S(2)}) collective-permute-start(f32[18,1024]{1,0:T(8,128)S(1)} %pad_maximum_fusion.1), channel_id=1, source_target_pairs={{1,2},{2,1},{5,6},{6,5},{9,10},{10,9},{13,14},{14,13},{17,18},{18,... | collective-permute-start | bytes 221192 | tf_op jit(solution)/shard_map/ppermute | solution.py:343
  8.3 0.7 copy-start.9
  9.0 0.6 copy-start.10
  20.4 6.3 %collective-permute-start.4 = (f32[8,128]{1,0:T(8,128)}, f32[8,128]{1,0:T(8,128)S(1)}, u32[]{:S(2)}, u32[]{:S(2)}) collective-permute-start(f32[8,128]{1,0:T(8,128)} %get-tuple-element.12), channel_id=1, source_target_pairs={{0,3},{1,2},{2,1},{3,0},{4,7},{5,6},{6,5},{7,4},{8,11},{9,10},{10,... | collective-permute-start | bytes 12296 | tf_op jit(solution)/shard_map/ppermute | solution.py:280
  24.3 4.7 %collective-permute-start.3 = (f32[8,128]{1,0:T(8,128)}, f32[8,128]{1,0:T(8,128)S(1)}, u32[]{:S(2)}, u32[]{:S(2)}) collective-permute-start(f32[8,128]{1,0:T(8,128)} %get-tuple-element.12), channel_id=1, source_target_pairs={{0,2},{1,3},{2,0},{3,1},{4,6},{5,7},{6,4},{7,5},{8,10},{9,11},{10,... | collective-permute-start | bytes 12296 | tf_op jit(solution)/shard_map/ppermute | solution.py:280
  26.2 3.8 %collective-permute-start.2 = (f32[8,128]{1,0:T(8,128)}, f32[8,128]{1,0:T(8,128)S(1)}, u32[]{:S(2)}, u32[]{:S(2)}) collective-permute-start(f32[8,128]{1,0:T(8,128)} %get-tuple-element.12), channel_id=1, source_target_pairs={{0,1},{1,0},{2,3},{3,2},{4,5},{5,4},{6,7},{7,6},{8,9},{9,8},{10,11... | collective-permute-start | bytes 12296 | tf_op jit(solution)/shard_map/ppermute | solution.py:280
  36.3 6.9 %collective-permute-start.6 = (f32[9,8,1024]{2,1,0:T(8,128)}, f32[9,8,1024]{2,1,0:T(8,128)S(1)}, u32[]{:S(2)}, u32[]{:S(2)}) collective-permute-start(f32[9,8,1024]{2,1,0:T(8,128)} %moment.1.refs_0_), channel_id=1, source_target_pairs={{0,16},{4,20},{8,24},{12,28},{16,0},{20,4},{24,8},{28,12},{1,17},{... | collective-permute-start | bytes 884744 | tf_op jit(solution)/shard_map/ppermute | solution.py:291
  37.9 8.7 %collective-permute-start.5 = (f32[9,8,1024]{2,1,0:T(8,128)}, f32[9,8,1024]{2,1,0:T(8,128)S(1)}, u32[]{:S(2)}, u32[]{:S(2)}) collective-permute-start(f32[9,8,1024]{2,1,0:T(8,128)} %moment.1.refs_0_), channel_id=1, source_target_pairs={{0,8},{4,12},{8,0},{12,4},{16,24},{20,28},{24,16},{28,20},{1,9},{5... | collective-permute-start | bytes 884744 | tf_op jit(solution)/shard_map/ppermute | solution.py:291
  43.3 10.7 %copy-start = (f32[9,8,1024]{2,1,0:T(8,128)}, f32[9,8,1024]{2,1,0:T(8,128)S(1)}, u32[]{:S(2)}) copy-start(f32[9,8,1024]{2,1,0:T(8,128)S(1)} %collective-permute-done.6.refs_2_) | copy-start | bytes 884740
  43.3 5.4 %collective-permute-start.8 = (f32[5,8,1024]{2,1,0:T(8,128)S(1)}, f32[5,8,1024]{2,1,0:T(8,128)S(1)}, u32[]{:S(2)}, u32[]{:S(2)}) collective-permute-start(f32[5,8,1024]{2,1,0:T(8,128)S(1)} %slice.17), channel_id=1, source_target_pairs={{0,8},{4,12},{8,0},{12,4},{16,24},{20,28},{24,16},{28,20},{1,9},{5... | collective-permute-start | bytes 491528 | tf_op jit(solution)/shard_map/ppermute | solution.py:291
  44.9 7.7 %collective-permute-start.9 = (f32[9,8,1024]{2,1,0:T(8,128)}, f32[9,8,1024]{2,1,0:T(8,128)S(1)}, u32[]{:S(2)}, u32[]{:S(2)}) collective-permute-start(f32[9,8,1024]{2,1,0:T(8,128)} %moment.1.refs_0_), channel_id=1, source_target_pairs={{0,4},{4,0},{8,12},{12,8},{16,20},{20,16},{24,28},{28,24},{1,5},{5... | collective-permute-start | bytes 884744 | tf_op jit(solution)/shard_map/ppermute | solution.py:291
  44.9 9.0 %collective-permute-start.11 = (f32[9,8,1024]{2,1,0:T(8,128)S(1)}, f32[9,8,1024]{2,1,0:T(8,128)S(1)}, u32[]{:S(2)}, u32[]{:S(2)}) collective-permute-start(f32[9,8,1024]{2,1,0:T(8,128)S(1)} %collective-permute-done.6.refs_2_), channel_id=1, source_target_pairs={{0,4},{4,0},{8,12},{12,8},{16,20},{20,16},{24,28},{28,24},{1,5},{5... | collective-permute-start | bytes 884744 | tf_op jit(solution)/shard_map/ppermute | solution.py:291
  46.6 7.4 %copy-start.1 = (f32[9,8,1024]{2,1,0:T(8,128)}, f32[9,8,1024]{2,1,0:T(8,128)S(1)}, u32[]{:S(2)}) copy-start(f32[9,8,1024]{2,1,0:T(8,128)S(1)} %collective-permute-done.5.refs_1_) | copy-start | bytes 884740
  46.6 7.4 %collective-permute-start.10 = (f32[9,8,1024]{2,1,0:T(8,128)S(1)}, f32[9,8,1024]{2,1,0:T(8,128)S(1)}, u32[]{:S(2)}, u32[]{:S(2)}) collective-permute-start(f32[9,8,1024]{2,1,0:T(8,128)S(1)} %collective-permute-done.5.refs_1_), channel_id=1, source_target_pairs={{0,4},{4,0},{8,12},{12,8},{16,20},{20,16},{24,28},{28,24},{1,5},{5... | collective-permute-start | bytes 884744 | tf_op jit(solution)/shard_map/ppermute | solution.py:291
  46.6 6.0 %collective-permute-start.7 = (f32[4,8,1024]{2,1,0:T(8,128)S(1)}, f32[4,8,1024]{2,1,0:T(8,128)S(1)}, u32[]{:S(2)}, u32[]{:S(2)}) collective-permute-start(f32[4,8,1024]{2,1,0:T(8,128)S(1)} %slice.16), channel_id=1, source_target_pairs={{0,16},{4,20},{8,24},{12,28},{16,0},{20,4},{24,8},{28,12},{1,17},{... | collective-permute-start | bytes 393224 | tf_op jit(solution)/shard_map/ppermute | solution.py:291
  48.7 5.3 %copy-start.5 = (f32[5,8,1024]{2,1,0:T(8,128)}, f32[5,8,1024]{2,1,0:T(8,128)S(1)}, u32[]{:S(2)}) copy-start(f32[5,8,1024]{2,1,0:T(8,128)S(1)} %collective-permute-done.8.refs_4_) | copy-start | bytes 491524
  48.7 5.2 %collective-permute-start.13 = (f32[5,8,1024]{2,1,0:T(8,128)S(1)}, f32[5,8,1024]{2,1,0:T(8,128)S(1)}, u32[]{:S(2)}, u32[]{:S(2)}) collective-permute-start(f32[5,8,1024]{2,1,0:T(8,128)S(1)} %collective-permute-done.8.refs_4_), channel_id=1, source_target_pairs={{0,4},{4,0},{8,12},{12,8},{16,20},{20,16},{24,28},{28,24},{1,5},{5... | collective-permute-start | bytes 491528 | tf_op jit(solution)/shard_map/ppermute | solution.py:291
  52.5 1.4 %copy-start.7 = (f32[4,8,1024]{2,1,0:T(8,128)}, f32[4,8,1024]{2,1,0:T(8,128)S(1)}, u32[]{:S(2)}) copy-start(f32[4,8,1024]{2,1,0:T(8,128)S(1)} %collective-permute-done.7.refs_3_) | copy-start | bytes 393220
  52.5 1.3 %collective-permute-start.12 = (f32[4,8,1024]{2,1,0:T(8,128)S(1)}, f32[4,8,1024]{2,1,0:T(8,128)S(1)}, u32[]{:S(2)}, u32[]{:S(2)}) collective-permute-start(f32[4,8,1024]{2,1,0:T(8,128)S(1)} %collective-permute-done.7.refs_3_), channel_id=1, source_target_pairs={{0,4},{4,0},{8,12},{12,8},{16,20},{20,16},{24,28},{28,24},{1,5},{5... | collective-permute-start | bytes 393224 | tf_op jit(solution)/shard_map/ppermute | solution.py:291
  52.6 1.4 %copy-start.2 = (f32[9,8,1024]{2,1,0:T(8,128)}, f32[9,8,1024]{2,1,0:T(8,128)S(1)}, u32[]{:S(2)}) copy-start(f32[9,8,1024]{2,1,0:T(8,128)S(1)} %collective-permute-done.9.refs_5_) | copy-start | bytes 884740
  53.9 0.7 copy-start.8
  53.9 0.8 %copy-start.3 = (f32[9,8,1024]{2,1,0:T(8,128)}, f32[9,8,1024]{2,1,0:T(8,128)S(1)}, u32[]{:S(2)}) copy-start(f32[9,8,1024]{2,1,0:T(8,128)S(1)} %collective-permute-done.11.refs_7_) | copy-start | bytes 884740
  53.9 0.9 %copy-start.4 = (f32[9,8,1024]{2,1,0:T(8,128)}, f32[9,8,1024]{2,1,0:T(8,128)S(1)}, u32[]{:S(2)}) copy-start(f32[9,8,1024]{2,1,0:T(8,128)S(1)} %collective-permute-done.10.refs_6_) | copy-start | bytes 884740
  54.8 0.7 copy-start.6
  59.4 6.0 %collective-permute-start.16 = (f32[64,128]{1,0:T(8,128)}, f32[64,128]{1,0:T(8,128)S(1)}, u32[]{:S(2)}, u32[]{:S(2)}) collective-permute-start(f32[64,128]{1,0:T(8,128)} %get-tuple-element.14), channel_id=1, source_target_pairs={{0,3},{1,2},{2,1},{3,0},{4,7},{5,6},{6,5},{7,4},{8,11},{9,10},{10,... | collective-permute-start | bytes 98312 | tf_op jit(solution)/shard_map/ppermute | solution.py:280
  62.2 5.0 %collective-permute-start.15 = (f32[64,128]{1,0:T(8,128)}, f32[64,128]{1,0:T(8,128)S(1)}, u32[]{:S(2)}, u32[]{:S(2)}) collective-permute-start(f32[64,128]{1,0:T(8,128)} %get-tuple-element.14), channel_id=1, source_target_pairs={{0,2},{1,3},{2,0},{3,1},{4,6},{5,7},{6,4},{7,5},{8,10},{9,11},{10,... | collective-permute-start | bytes 98312 | tf_op jit(solution)/shard_map/ppermute | solution.py:280
  62.2 5.0 %collective-permute-start.14 = (f32[64,128]{1,0:T(8,128)}, f32[64,128]{1,0:T(8,128)S(1)}, u32[]{:S(2)}, u32[]{:S(2)}) collective-permute-start(f32[64,128]{1,0:T(8,128)} %get-tuple-element.14), channel_id=1, source_target_pairs={{0,1},{1,0},{2,3},{3,2},{4,5},{5,4},{6,7},{7,6},{8,9},{9,8},{10,11... | collective-permute-start | bytes 98312 | tf_op jit(solution)/shard_map/ppermute | solution.py:280

commit v3 on v2

--- a/solution.py
+++ b/solution.py
@@ -84,7 +84,7 @@
     return diag_re * scaled, -shift_im * scaled
 
 
-def krylov_kernel(where, nodes_ref, own, pot, paired, other, blocks, b_ref, wide, sums, u, v, inv, onsite):
+def krylov_kernel(where, node, own, pot, paired, other, blocks, b_ref, wide, sums, u, v, inv, onsite):
     k = pl.program_id(0)
     count = pl.num_programs(0)
     planes, cols, cells = own.shape
@@ -115,13 +115,14 @@
         for z in range(planes + 4):
             wide[z] = jnp.broadcast_to(onsite[z : z + 1, :], (cols, cells))
 
-    inv_re, inv_im = inverses(onsite[...], nodes_ref[k, 0], nodes_ref[k, 1])
-    for z in range(planes + 4):
-        inv[0, z] = jnp.broadcast_to(inv_re[z : z + 1], (cols, cells))
-        inv[1, z] = jnp.broadcast_to(inv_im[z : z + 1], (cols, cells))
-
     def at(j):
         return slice(j * LANES, (j + 1) * LANES)
+
+    for j in range(vecs):
+        inv_re, inv_im = inverses(onsite[:, at(j)], node[0, 0:1, :], node[0, 1:2, :])
+        for z in range(planes + 4):
+            inv[0, z, :, at(j)] = jnp.broadcast_to(inv_re[z : z + 1], (cols, LANES))
+            inv[1, z, :, at(j)] = jnp.broadcast_to(inv_im[z : z + 1], (cols, LANES))
 
     def factor(c, z, j):
         return inv[c, z, :, at(j)]
@@ -244,23 +245,28 @@
 
 
 def gram_kernel(where, pot, *refs, layout, scale):
-    pieces, out, gram, edge = refs[: len(layout)], refs[-3], refs[-2], refs[-1]
+    pieces = refs[: len(layout)]
+    out, gram, field, sems = refs[len(layout) :]
     planes, width, cells = out.shape
-    for ref, (mask, first) in zip(pieces, layout):
-        cols = ref.shape[1]
+    arrivals = []
+    for i, (ref, (mask, first)) in enumerate(zip(pieces, layout)):
+        count, cols = ref.shape[:2]
         start = 0 if cols == width else pl.multiple_of((where[0] ^ mask) * cols, cols)
-        for z in range(ref.shape[0]):
-            if first + z < planes:
-                out[first + z, pl.ds(start, cols), :] = ref[z]
-            else:
-                edge[pl.ds(start, cols), :] = ref[z]
+        target = field.at[pl.ds(first, count), pl.ds(start, cols), :]
+        arrivals.append(pltpu.make_async_copy(ref, target, sems.at[i]))
+    for copy in arrivals:
+        copy.start()
+    for copy in arrivals:
+        copy.wait()
+    leave = pltpu.make_async_copy(field.at[pl.ds(0, planes)], out, sems.at[len(layout)])
+    leave.start()
     cell = lax.broadcasted_iota(jnp.int32, (1, cells), 1)
     x_ok = (cell < cells - NY).astype(jnp.float32)
     y_ok = (cell % NY != NY - 1).astype(jnp.float32)
     total = jnp.zeros((2 * width, 4 * width), jnp.float32)
     for z in range(planes):
-        s = out[z]
-        after = out[z + 1] if z + 1 < planes else edge[...]
+        s = field[z]
+        after = field[z + 1]
         beside = pltpu.roll(s, cells - NY, 1) * x_ok + pltpu.roll(s, cells - 1, 1) * y_ok + after
         applied = (3.0 + 0.5 * pot[z : z + 1, :]) * s - beside
         s_high, s_low = halves(s)
@@ -271,7 +277,11 @@
             left, right, (((1,), (1,)), ((), ())), preferred_element_type=jnp.float32
         )
     both = total[:width, : 2 * width] + total[:width, 2 * width :] + total[width:, : 2 * width]
-    gram[...] = both * scale
+    both = both * scale
+    half = both[:, :width]
+    gram[:, :width] = half + half.T
+    gram[:, width:] = both[:, width:]
+    leave.wait()
 
 
 def butterfly(x, axis):
@@ -319,6 +329,7 @@
         [[CENTRE + RADIUS * math.cos(a), RADIUS * math.sin(a)] for a in angles], np.float32
     )
     shifts = np.ascontiguousarray(np.broadcast_to(table.T[:, :, None], (2, nodes, LANES)))
+    rows = np.ascontiguousarray(np.broadcast_to(table[:, :, None], (nodes, 2, LANES)))
     spare = [0.0] * (LANES - nodes)
     weights = jnp.array(
         [
@@ -360,7 +371,7 @@
             num_scalar_prefetch=1,
             grid=(nodes,),
             in_specs=[
-                smem,
+                pl.BlockSpec((1, 2, LANES), lambda k, w: (k, 0, 0)),
                 own_spec,
                 full(potential.shape),
                 full(paired.shape),
@@ -386,7 +397,7 @@
             jax.ShapeDtypeStruct((cols, LANES), f32),
         ],
         name="krylov",
-    )(where, table, source, potential, paired, other)
+    )(where, rows, source, potential, paired, other)
 
     totals = butterfly(sums, "dom")
 
@@ -413,21 +424,24 @@
     held = spread(own)
     layout = tuple((mask, first) for mask, first, _ in held)
     vmem = pl.BlockSpec(memory_space=pltpu.VMEM)
+    hbm = pl.BlockSpec(memory_space=pl.ANY)
     scale = 1.0 / (cells * planes * slabs)
     subspace, gram = pl.pallas_call(
         functools.partial(gram_kernel, layout=layout, scale=scale),
-        in_specs=[smem] + [vmem] * (1 + len(held)),
-        out_specs=[vmem, vmem],
+        in_specs=[smem, vmem] + [hbm] * len(held),
+        out_specs=[hbm, vmem],
         out_shape=[
             jax.ShapeDtypeStruct((planes, width, cells), f32),
             jax.ShapeDtypeStruct((width, 2 * width), f32),
         ],
-        scratch_shapes=[pltpu.VMEM((width, cells), f32)],
+        scratch_shapes=[
+            pltpu.VMEM((planes + 1, width, cells), f32),
+            pltpu.SemaphoreType.DMA((len(held) + 1,)),
+        ],
         name="gram",
     )(where, potential, *[piece for _, _, piece in held])
     gram = butterfly(gram, "dom")
-    part_h = gram[:, :width]
-    return subspace, part_h + part_h.T, gram[:, width:]
+    return subspace, gram[:, :width], gram[:, width:]
 
 
 def solution(mesh):

time: 69.3 us -> 69.9 us (level)
  other arithmetic: 3.39 us -> 2.69 us
    pallas_call x1, Pallas kernels: 3.94 us -> 4.7 us  [on_device(): pl.pallas_call(functools.partial(gram_kernel, layout=layout, scale=scale)...]
    slice x1 -> x0, other arithmetic: 0.7 us -> none  [on_device(): return (subspace, part_h + part_h.T, gram[:, width:])]
where the time goes in v3:
time: 69.9 us; the launch traced here: 69.3 us
  Pallas kernels  20.3 us (29%)
  starting transfers between devices  20.2 us (29%)
  waiting for transfers between devices  20.1 us (29%)
  local copies, waits for them, and re-layouts  5.25 us (8%)
  other arithmetic  2.69 us (4%)
  between operations  0.8 us (1%)
    ppermute x9, waiting for transfers between devices, swap(): return lax.ppermute(x, 'shift', [(i, i ^ mask) for i in range(count)])  11.8 us
    ppermute x6, starting transfers between devices, butterfly(): lax.ppermute(x, axis, [(i, i ^ m) for i in range(4)])  10.8 us
    pallas_call x1, Pallas kernels, on_device(): pl.pallas_call(krylov_kernel, grid_spec=pltpu.PrefetchScalarGridSpec(num_...  10.6 us
    ppermute x6, waiting for transfers between devices, butterfly(): lax.ppermute(x, axis, [(i, i ^ m) for i in range(4)])  6.81 us
    ppermute x9, starting transfers between devices, swap(): return lax.ppermute(x, 'shift', [(i, i ^ mask) for i in range(count)])  5.66 us
    pallas_call x1, Pallas kernels, on_device(): pl.pallas_call(moment_kernel, grid=((planes + 1) // group,), in_specs=[fu...  5.01 us
    pallas_call x1, Pallas kernels, on_device(): pl.pallas_call(functools.partial(gram_kernel, layout=layout, scale=scale)...  4.7 us
    ppermute x1, starting transfers between devices, on_device(): paired = lax.ppermute(edge(jnp.where(even, planes - 2, 0)), 'dom', pairs(0))  3.12 us
  transfers between devices with their start and end apart: 17, of which 10 were waited for; matrix products, arithmetic and copies ran while one was open for 1% of the time, Pallas kernels for 0%

profile of v3, /device:TPU:0, one launch (start us, length us, event | category | flops | bytes accessed | tf_op | source)
XLA Modules:
  0.0 69.3 jit_solution(15860108798132475278)
XLA Ops:
  0.7 0.8 %constant_dynamic-slice_fusion = (f32[2,1024]{1,0:T(2,128)S(1)}, f32[2,1024]{1,0:T(2,128)S(1)}) fusion(f32[8,1024]{1,0:T(8,128)} %pot.3, s32[]{:T(128)S(6)} %select_n.27, s32[]{:T(128)S(6)} %select_n.25), kind=kLoop, calls=%fused_computation.6 | loop fusion | bytes 32776 | tf_op jit(solution)/shard_map/dynamic_slice | solution.py:345
  1.5 0.9 %dynamic-slice_bitcast_fusion = (f32[16,1024]{1,0:T(8,128)S(1)}, f32[16,1024]{1,0:T(8,128)S(1)}) fusion(f32[8,64,1024]{2,1,0:T(8,128)} %own.1, s32[]{:T(128)S(6)} %select_n.27, s32[]{:T(128)S(6)} %select_n.26, s32[]{:T(128)S(6)} %select_n.25), kind=kLoop, calls=%fused_computation.2 | loop fusion | bytes 262156 | tf_op jit(solution)/shard_map/reshape | solution.py:346
  2.4 3.1 %collective-permute-start = (f32[18,1024]{1,0:T(8,128)S(1)}, f32[18,1024]{1,0:T(8,128)S(1)}, u32[]{:S(2)}, u32[]{:S(2)}) collective-permute-start(f32[18,1024]{1,0:T(8,128)S(1)} %pad_maximum_fusion), channel_id=1, source_target_pairs={{0,1},{2,3},{1,0},{3,2},{4,5},{6,7},{5,4},{7,6},{8,9},{10,11},{9,8... | collective-permute-start | bytes 221192 | tf_op jit(solution)/shard_map/ppermute | solution.py:353
  5.5 0.7 collective-permute-start.1
  6.2 0.6 pad_add_fusion.where
  6.8 1.5 %collective-permute-done.paired = f32[18,1024]{1,0:T(8,128)S(1)} collective-permute-done((f32[18,1024]{1,0:T(8,128)S(1)}, f32[18,1024]{1,0:T(8,128)S(1)}, u32[]{:S(2)}, u32[]{:S(2)}) %collective-permute-start) | collective-permute-done | bytes 73760 | tf_op jit(solution)/shard_map/ppermute | solution.py:353
  8.3 0.6 copy-done.9
  9.0 0.6 copy-done.10
  9.6 10.6 %krylov.1 = (f32[8,2,9,8,1024]{4,3,2,1,0:T(8,128)}, f32[12,8,1024]{2,1,0:T(8,128)}, f32[12,8,1024]{2,1,0:T(8,128)}, f32[8,128]{1,0:T(8,128)}) custom-call(s32[4]{0:T(128)} %pad_add_fusion.where, f32[8,2,128]{2,1,0:T(2,128)} %constant.42.clone.node, f32[8,64,1024]{2,1,0:T(8,128)} %own.1, f32[8,1024]{1,0:T(8,128)} %pot.3, f32[18,1024]{1,0:T(8,128)} %copy-done.9, ...), custom_call_target="tpu_custom_call" | custom-call | tf_op jit(solution)/shard_map/krylov/pallas_call | solution.py:368
  20.2 3.9 %collective-permute-start.4 = (f32[8,128]{1,0:T(8,128)}, f32[8,128]{1,0:T(8,128)S(1)}, u32[]{:S(2)}, u32[]{:S(2)}) collective-permute-start(f32[8,128]{1,0:T(8,128)} %get-tuple-element.12), channel_id=1, source_target_pairs={{0,3},{1,2},{2,1},{3,0},{4,7},{5,6},{6,5},{7,4},{8,11},{9,10},{10,... | collective-permute-start | bytes 12296 | tf_op jit(solution)/shard_map/ppermute | solution.py:290
  24.1 1.9 %collective-permute-start.3 = (f32[8,128]{1,0:T(8,128)}, f32[8,128]{1,0:T(8,128)S(1)}, u32[]{:S(2)}, u32[]{:S(2)}) collective-permute-start(f32[8,128]{1,0:T(8,128)} %get-tuple-element.12), channel_id=1, source_target_pairs={{0,2},{1,3},{2,0},{3,1},{4,6},{5,7},{6,4},{7,5},{8,10},{9,11},{10,... | collective-permute-start | bytes 12296 | tf_op jit(solution)/shard_map/ppermute | solution.py:290
  26.5 2.3 %collective-permute-done.3 = f32[8,128]{1,0:T(8,128)S(1)} collective-permute-done((f32[8,128]{1,0:T(8,128)}, f32[8,128]{1,0:T(8,128)S(1)}, u32[]{:S(2)}, u32[]{:S(2)}) %collective-permute-start.3) | collective-permute-done | bytes 4128 | tf_op jit(solution)/shard_map/ppermute | solution.py:290
  28.8 1.0 %collective-permute-done.2 = f32[8,128]{1,0:T(8,128)S(1)} collective-permute-done((f32[8,128]{1,0:T(8,128)}, f32[8,128]{1,0:T(8,128)S(1)}, u32[]{:S(2)}, u32[]{:S(2)}) %collective-permute-start.2) | collective-permute-done | bytes 4128 | tf_op jit(solution)/shard_map/ppermute | solution.py:290
  29.8 1.3 %add_add_fusion.1.sums = f32[8,128]{1,0:T(8,128)} fusion(f32[8,128]{1,0:T(8,128)S(1)} %collective-permute-done.3, f32[8,128]{1,0:T(8,128)S(1)} %collective-permute-done.4, f32[8,128]{1,0:T(8,128)} %get-tuple-element.12, f32[8,128]{1,0:T(8,128)S(1)} %collective-permute-done.2), kind=kLoop, calls=%fused_computation.5 | loop fusion | flops 3072 | bytes 20480 | tf_op jit(solution)/shard_map/add | solution.py:291
  31.1 5.0 %moment.1.refs_0_ = f32[9,8,1024]{2,1,0:T(8,128)} custom-call(f32[2,8,128]{2,1,0:T(8,128)} %constant.43.clone.shifts, f32[2,128]{1,0:T(2,128)} %constant.41.clone.weights, f32[8,2,9,8,1024]{4,3,2,1,0:T(8,128)} %get-tuple-element.9.blocks, f32[12,8,1024]{2,1,0:T(8,128)} %get-tuple-element.10.b_ref, f32[12,8,1024]{2,1,0:T(8,128)} %get-tuple-element.11.onsite, ...), custom_call_target="tpu_custom_call" | custom-call | tf_op jit(solution)/shard_map/moment/pallas_call | solution.py:405
  36.1 1.5 %collective-permute-start.6 = (f32[9,8,1024]{2,1,0:T(8,128)}, f32[9,8,1024]{2,1,0:T(8,128)S(1)}, u32[]{:S(2)}, u32[]{:S(2)}) collective-permute-start(f32[9,8,1024]{2,1,0:T(8,128)} %moment.1.refs_0_), channel_id=1, source_target_pairs={{0,16},{4,20},{8,24},{12,28},{16,0},{20,4},{24,8},{28,12},{1,17},{... | collective-permute-start | bytes 884744 | tf_op jit(solution)/shard_map/ppermute | solution.py:301
  37.6 1.5 %collective-permute-start.5 = (f32[9,8,1024]{2,1,0:T(8,128)}, f32[9,8,1024]{2,1,0:T(8,128)S(1)}, u32[]{:S(2)}, u32[]{:S(2)}) collective-permute-start(f32[9,8,1024]{2,1,0:T(8,128)} %moment.1.refs_0_), channel_id=1, source_target_pairs={{0,8},{4,12},{8,0},{12,4},{16,24},{20,28},{24,16},{28,20},{1,9},{5... | collective-permute-start | bytes 884744 | tf_op jit(solution)/shard_map/ppermute | solution.py:301
  39.1 3.9 %collective-permute-done.6.refs_2_ = f32[9,8,1024]{2,1,0:T(8,128)S(1)} collective-permute-done((f32[9,8,1024]{2,1,0:T(8,128)}, f32[9,8,1024]{2,1,0:T(8,128)S(1)}, u32[]{:S(2)}, u32[]{:S(2)}) %collective-permute-start.6) | collective-permute-done | bytes 294944 | tf_op jit(solution)/shard_map/ppermute | solution.py:301
  43.1 1.6 %collective-permute-start.8 = (f32[5,8,1024]{2,1,0:T(8,128)S(1)}, f32[5,8,1024]{2,1,0:T(8,128)S(1)}, u32[]{:S(2)}, u32[]{:S(2)}) collective-permute-start(f32[5,8,1024]{2,1,0:T(8,128)S(1)} %slice.17), channel_id=1, source_target_pairs={{0,8},{4,12},{8,0},{12,4},{16,24},{20,28},{24,16},{28,20},{1,9},{5... | collective-permute-start | bytes 491528 | tf_op jit(solution)/shard_map/ppermute | solution.py:301
  45.1 1.2 %collective-permute-done.5.refs_1_ = f32[9,8,1024]{2,1,0:T(8,128)S(1)} collective-permute-done((f32[9,8,1024]{2,1,0:T(8,128)}, f32[9,8,1024]{2,1,0:T(8,128)S(1)}, u32[]{:S(2)}, u32[]{:S(2)}) %collective-permute-start.5) | collective-permute-done | bytes 294944 | tf_op jit(solution)/shard_map/ppermute | solution.py:301
  46.3 0.6 collective-permute-start.7
  46.9 1.5 %collective-permute-done.8.refs_4_ = f32[5,8,1024]{2,1,0:T(8,128)S(1)} collective-permute-done((f32[5,8,1024]{2,1,0:T(8,128)S(1)}, f32[5,8,1024]{2,1,0:T(8,128)S(1)}, u32[]{:S(2)}, u32[]{:S(2)}) %collective-permute-start.8) | collective-permute-done | bytes 163872 | tf_op jit(solution)/shard_map/ppermute | solution.py:301
  48.5 3.9 %collective-permute-done.7.refs_3_ = f32[4,8,1024]{2,1,0:T(8,128)S(1)} collective-permute-done((f32[4,8,1024]{2,1,0:T(8,128)S(1)}, f32[4,8,1024]{2,1,0:T(8,128)S(1)}, u32[]{:S(2)}, u32[]{:S(2)}) %collective-permute-start.7) | collective-permute-done | bytes 131104 | tf_op jit(solution)/shard_map/ppermute | solution.py:301
  52.3 1.3 %collective-permute-done.12.refs_8_ = f32[4,8,1024]{2,1,0:T(8,128)S(1)} collective-permute-done((f32[4,8,1024]{2,1,0:T(8,128)S(1)}, f32[4,8,1024]{2,1,0:T(8,128)S(1)}, u32[]{:S(2)}, u32[]{:S(2)}) %collective-permute-start.12) | collective-permute-done | bytes 131104 | tf_op jit(solution)/shard_map/ppermute | solution.py:301
  54.6 0.7 copy-done.6
  55.2 4.7 %gram.1 = (f32[8,64,1024]{2,1,0:T(8,128)}, f32[64,128]{1,0:T(8,128)}) custom-call(s32[4]{0:T(128)} %pad_add_fusion.where, f32[8,1024]{1,0:T(8,128)} %pot.3, f32[9,8,1024]{2,1,0:T(8,128)} %moment.1.refs_0_, f32[9,8,1024]{2,1,0:T(8,128)} %copy-done.1, f32[9,8,1024]{2,1,0:T(8,128)} %copy-done, f32[4,8,1024]{2,1,0:T(8,128)} %copy-done.7, ...), custom_call_target="tpu_custom_call" | custom-call | tf_op jit(solution)/shard_map/gram/pallas_call | solution.py:429
  59.9 2.9 %collective-permute-start.16 = (f32[64,128]{1,0:T(8,128)}, f32[64,128]{1,0:T(8,128)S(1)}, u32[]{:S(2)}, u32[]{:S(2)}) collective-permute-start(f32[64,128]{1,0:T(8,128)} %get-tuple-element.14), channel_id=1, source_target_pairs={{0,3},{1,2},{2,1},{3,0},{4,7},{5,6},{6,5},{7,4},{8,11},{9,10},{10,... | collective-permute-start | bytes 98312 | tf_op jit(solution)/shard_map/ppermute | solution.py:290
  62.9 1.5 %collective-permute-start.14 = (f32[64,128]{1,0:T(8,128)}, f32[64,128]{1,0:T(8,128)S(1)}, u32[]{:S(2)}, u32[]{:S(2)}) collective-permute-start(f32[64,128]{1,0:T(8,128)} %get-tuple-element.14), channel_id=1, source_target_pairs={{0,1},{1,0},{2,3},{3,2},{4,5},{5,4},{6,7},{7,6},{8,9},{9,8},{10,11... | collective-permute-start | bytes 98312 | tf_op jit(solution)/shard_map/ppermute | solution.py:290
  64.4 1.6 %collective-permute-done.16 = f32[64,128]{1,0:T(8,128)S(1)} collective-permute-done((f32[64,128]{1,0:T(8,128)}, f32[64,128]{1,0:T(8,128)S(1)}, u32[]{:S(2)}, u32[]{:S(2)}) %collective-permute-start.16) | collective-permute-done | bytes 32800 | tf_op jit(solution)/shard_map/ppermute | solution.py:290
  66.0 1.8 %collective-permute-done.15 = f32[64,128]{1,0:T(8,128)S(1)} collective-permute-done((f32[64,128]{1,0:T(8,128)}, f32[64,128]{1,0:T(8,128)S(1)}, u32[]{:S(2)}, u32[]{:S(2)}) %collective-permute-start.15) | collective-permute-done | bytes 32800 | tf_op jit(solution)/shard_map/ppermute | solution.py:290
  67.9 0.8 %add_add_fusion = f32[64,128]{1,0:T(8,128)S(1)} fusion(f32[64,128]{1,0:T(8,128)S(1)} %collective-permute-done.15, f32[64,128]{1,0:T(8,128)S(1)} %collective-permute-done.16, f32[64,128]{1,0:T(8,128)} %get-tuple-element.14, f32[64,128]{1,0:T(8,128)S(1)} %collective-permute-done.14), kind=kLoop, calls=%fused_computation.4 | loop fusion | flops 24576 | bytes 163840 | tf_op jit(solution)/shard_map/add | solution.py:291
  68.7 0.7 %fusion = (f32[64,64]{1,0:T(8,128)}, f32[64,64]{1,0:T(8,128)}) fusion(f32[64,128]{1,0:T(8,128)S(1)} %add_add_fusion), kind=kLoop, calls=%fused_computation.9 | loop fusion | bytes 65536 | tf_op jit(solution)/shard_map/slice | solution.py:444
  (37 shorter events, 1.9 us)
Async XLA Ops:
  2.4 5.9 %collective-permute-start = (f32[18,1024]{1,0:T(8,128)S(1)}, f32[18,1024]{1,0:T(8,128)S(1)}, u32[]{:S(2)}, u32[]{:S(2)}) collective-permute-start(f32[18,1024]{1,0:T(8,128)S(1)} %pad_maximum_fusion), channel_id=1, source_target_pairs={{0,1},{2,3},{1,0},{3,2},{4,5},{6,7},{5,4},{7,6},{8,9},{10,11},{9,8... | collective-permute-start | bytes 221192 | tf_op jit(solution)/shard_map/ppermute | solution.py:353
  5.5 2.8 %collective-permute-start.1 = (f32[18,1024]{1,0:T(8,128)S(1)}, f32[18,1024]{1,0:T(8,128)S(1)}, u32[]{:S(2)}, u32[]{:S(2)}) collective-permute-start(f32[18,1024]{1,0:T(8,128)S(1)} %pad_maximum_fusion.1), channel_id=1, source_target_pairs={{1,2},{2,1},{5,6},{6,5},{9,10},{10,9},{13,14},{14,13},{17,18},{18,... | collective-permute-start | bytes 221192 | tf_op jit(solution)/shard_map/ppermute | solution.py:354
  8.3 0.7 copy-start.9
  9.0 0.6 copy-start.10
  20.2 6.3 %collective-permute-start.4 = (f32[8,128]{1,0:T(8,128)}, f32[8,128]{1,0:T(8,128)S(1)}, u32[]{:S(2)}, u32[]{:S(2)}) collective-permute-start(f32[8,128]{1,0:T(8,128)} %get-tuple-element.12), channel_id=1, source_target_pairs={{0,3},{1,2},{2,1},{3,0},{4,7},{5,6},{6,5},{7,4},{8,11},{9,10},{10,... | collective-permute-start | bytes 12296 | tf_op jit(solution)/shard_map/ppermute | solution.py:290
  24.1 4.7 %collective-permute-start.3 = (f32[8,128]{1,0:T(8,128)}, f32[8,128]{1,0:T(8,128)S(1)}, u32[]{:S(2)}, u32[]{:S(2)}) collective-permute-start(f32[8,128]{1,0:T(8,128)} %get-tuple-element.12), channel_id=1, source_target_pairs={{0,2},{1,3},{2,0},{3,1},{4,6},{5,7},{6,4},{7,5},{8,10},{9,11},{10,... | collective-permute-start | bytes 12296 | tf_op jit(solution)/shard_map/ppermute | solution.py:290
  26.0 3.8 %collective-permute-start.2 = (f32[8,128]{1,0:T(8,128)}, f32[8,128]{1,0:T(8,128)S(1)}, u32[]{:S(2)}, u32[]{:S(2)}) collective-permute-start(f32[8,128]{1,0:T(8,128)} %get-tuple-element.12), channel_id=1, source_target_pairs={{0,1},{1,0},{2,3},{3,2},{4,5},{5,4},{6,7},{7,6},{8,9},{9,8},{10,11... | collective-permute-start | bytes 12296 | tf_op jit(solution)/shard_map/ppermute | solution.py:290
  36.1 6.9 %collective-permute-start.6 = (f32[9,8,1024]{2,1,0:T(8,128)}, f32[9,8,1024]{2,1,0:T(8,128)S(1)}, u32[]{:S(2)}, u32[]{:S(2)}) collective-permute-start(f32[9,8,1024]{2,1,0:T(8,128)} %moment.1.refs_0_), channel_id=1, source_target_pairs={{0,16},{4,20},{8,24},{12,28},{16,0},{20,4},{24,8},{28,12},{1,17},{... | collective-permute-start | bytes 884744 | tf_op jit(solution)/shard_map/ppermute | solution.py:301
  37.6 8.7 %collective-permute-start.5 = (f32[9,8,1024]{2,1,0:T(8,128)}, f32[9,8,1024]{2,1,0:T(8,128)S(1)}, u32[]{:S(2)}, u32[]{:S(2)}) collective-permute-start(f32[9,8,1024]{2,1,0:T(8,128)} %moment.1.refs_0_), channel_id=1, source_target_pairs={{0,8},{4,12},{8,0},{12,4},{16,24},{20,28},{24,16},{28,20},{1,9},{5... | collective-permute-start | bytes 884744 | tf_op jit(solution)/shard_map/ppermute | solution.py:301
  43.1 10.7 %copy-start = (f32[9,8,1024]{2,1,0:T(8,128)}, f32[9,8,1024]{2,1,0:T(8,128)S(1)}, u32[]{:S(2)}) copy-start(f32[9,8,1024]{2,1,0:T(8,128)S(1)} %collective-permute-done.6.refs_2_) | copy-start | bytes 884740
  43.1 5.4 %collective-permute-start.8 = (f32[5,8,1024]{2,1,0:T(8,128)S(1)}, f32[5,8,1024]{2,1,0:T(8,128)S(1)}, u32[]{:S(2)}, u32[]{:S(2)}) collective-permute-start(f32[5,8,1024]{2,1,0:T(8,128)S(1)} %slice.17), channel_id=1, source_target_pairs={{0,8},{4,12},{8,0},{12,4},{16,24},{20,28},{24,16},{28,20},{1,9},{5... | collective-permute-start | bytes 491528 | tf_op jit(solution)/shard_map/ppermute | solution.py:301
  44.6 7.7 %collective-permute-start.9 = (f32[9,8,1024]{2,1,0:T(8,128)}, f32[9,8,1024]{2,1,0:T(8,128)S(1)}, u32[]{:S(2)}, u32[]{:S(2)}) collective-permute-start(f32[9,8,1024]{2,1,0:T(8,128)} %moment.1.refs_0_), channel_id=1, source_target_pairs={{0,4},{4,0},{8,12},{12,8},{16,20},{20,16},{24,28},{28,24},{1,5},{5... | collective-permute-start | bytes 884744 | tf_op jit(solution)/shard_map/ppermute | solution.py:301
  44.6 9.0 %collective-permute-start.11 = (f32[9,8,1024]{2,1,0:T(8,128)S(1)}, f32[9,8,1024]{2,1,0:T(8,128)S(1)}, u32[]{:S(2)}, u32[]{:S(2)}) collective-permute-start(f32[9,8,1024]{2,1,0:T(8,128)S(1)} %collective-permute-done.6.refs_2_), channel_id=1, source_target_pairs={{0,4},{4,0},{8,12},{12,8},{16,20},{20,16},{24,28},{28,24},{1,5},{5... | collective-permute-start | bytes 884744 | tf_op jit(solution)/shard_map/ppermute | solution.py:301
  46.3 7.4 %copy-start.1 = (f32[9,8,1024]{2,1,0:T(8,128)}, f32[9,8,1024]{2,1,0:T(8,128)S(1)}, u32[]{:S(2)}) copy-start(f32[9,8,1024]{2,1,0:T(8,128)S(1)} %collective-permute-done.5.refs_1_) | copy-start | bytes 884740
  46.3 7.4 %collective-permute-start.10 = (f32[9,8,1024]{2,1,0:T(8,128)S(1)}, f32[9,8,1024]{2,1,0:T(8,128)S(1)}, u32[]{:S(2)}, u32[]{:S(2)}) collective-permute-start(f32[9,8,1024]{2,1,0:T(8,128)S(1)} %collective-permute-done.5.refs_1_), channel_id=1, source_target_pairs={{0,4},{4,0},{8,12},{12,8},{16,20},{20,16},{24,28},{28,24},{1,5},{5... | collective-permute-start | bytes 884744 | tf_op jit(solution)/shard_map/ppermute | solution.py:301
  46.3 6.0 %collective-permute-start.7 = (f32[4,8,1024]{2,1,0:T(8,128)S(1)}, f32[4,8,1024]{2,1,0:T(8,128)S(1)}, u32[]{:S(2)}, u32[]{:S(2)}) collective-permute-start(f32[4,8,1024]{2,1,0:T(8,128)S(1)} %slice.16), channel_id=1, source_target_pairs={{0,16},{4,20},{8,24},{12,28},{16,0},{20,4},{24,8},{28,12},{1,17},{... | collective-permute-start | bytes 393224 | tf_op jit(solution)/shard_map/ppermute | solution.py:301
  48.5 5.3 %copy-start.5 = (f32[5,8,1024]{2,1,0:T(8,128)}, f32[5,8,1024]{2,1,0:T(8,128)S(1)}, u32[]{:S(2)}) copy-start(f32[5,8,1024]{2,1,0:T(8,128)S(1)} %collective-permute-done.8.refs_4_) | copy-start | bytes 491524
  48.5 5.2 %collective-permute-start.13 = (f32[5,8,1024]{2,1,0:T(8,128)S(1)}, f32[5,8,1024]{2,1,0:T(8,128)S(1)}, u32[]{:S(2)}, u32[]{:S(2)}) collective-permute-start(f32[5,8,1024]{2,1,0:T(8,128)S(1)} %collective-permute-done.8.refs_4_), channel_id=1, source_target_pairs={{0,4},{4,0},{8,12},{12,8},{16,20},{20,16},{24,28},{28,24},{1,5},{5... | collective-permute-start | bytes 491528 | tf_op jit(solution)/shard_map/ppermute | solution.py:301
  52.3 1.4 %copy-start.7 = (f32[4,8,1024]{2,1,0:T(8,128)}, f32[4,8,1024]{2,1,0:T(8,128)S(1)}, u32[]{:S(2)}) copy-start(f32[4,8,1024]{2,1,0:T(8,128)S(1)} %collective-permute-done.7.refs_3_) | copy-start | bytes 393220
  52.3 1.3 %collective-permute-start.12 = (f32[4,8,1024]{2,1,0:T(8,128)S(1)}, f32[4,8,1024]{2,1,0:T(8,128)S(1)}, u32[]{:S(2)}, u32[]{:S(2)}) collective-permute-start(f32[4,8,1024]{2,1,0:T(8,128)S(1)} %collective-permute-done.7.refs_3_), channel_id=1, source_target_pairs={{0,4},{4,0},{8,12},{12,8},{16,20},{20,16},{24,28},{28,24},{1,5},{5... | collective-permute-start | bytes 393224 | tf_op jit(solution)/shard_map/ppermute | solution.py:301
  52.3 1.4 %copy-start.2 = (f32[9,8,1024]{2,1,0:T(8,128)}, f32[9,8,1024]{2,1,0:T(8,128)S(1)}, u32[]{:S(2)}) copy-start(f32[9,8,1024]{2,1,0:T(8,128)S(1)} %collective-permute-done.9.refs_5_) | copy-start | bytes 884740
  53.7 0.7 copy-start.8
  53.7 0.8 %copy-start.3 = (f32[9,8,1024]{2,1,0:T(8,128)}, f32[9,8,1024]{2,1,0:T(8,128)S(1)}, u32[]{:S(2)}) copy-start(f32[9,8,1024]{2,1,0:T(8,128)S(1)} %collective-permute-done.11.refs_7_) | copy-start | bytes 884740
  53.7 0.9 %copy-start.4 = (f32[9,8,1024]{2,1,0:T(8,128)}, f32[9,8,1024]{2,1,0:T(8,128)S(1)}, u32[]{:S(2)}) copy-start(f32[9,8,1024]{2,1,0:T(8,128)S(1)} %collective-permute-done.10.refs_6_) | copy-start | bytes 884740
  54.6 0.7 copy-start.6
  59.9 6.1 %collective-permute-start.16 = (f32[64,128]{1,0:T(8,128)}, f32[64,128]{1,0:T(8,128)S(1)}, u32[]{:S(2)}, u32[]{:S(2)}) collective-permute-start(f32[64,128]{1,0:T(8,128)} %get-tuple-element.14), channel_id=1, source_target_pairs={{0,3},{1,2},{2,1},{3,0},{4,7},{5,6},{6,5},{7,4},{8,11},{9,10},{10,... | collective-permute-start | bytes 98312 | tf_op jit(solution)/shard_map/ppermute | solution.py:290
  62.9 5.0 %collective-permute-start.15 = (f32[64,128]{1,0:T(8,128)}, f32[64,128]{1,0:T(8,128)S(1)}, u32[]{:S(2)}, u32[]{:S(2)}) collective-permute-start(f32[64,128]{1,0:T(8,128)} %get-tuple-element.14), channel_id=1, source_target_pairs={{0,2},{1,3},{2,0},{3,1},{4,6},{5,7},{6,4},{7,5},{8,10},{9,11},{10,... | collective-permute-start | bytes 98312 | tf_op jit(solution)/shard_map/ppermute | solution.py:290
  62.9 5.0 %collective-permute-start.14 = (f32[64,128]{1,0:T(8,128)}, f32[64,128]{1,0:T(8,128)S(1)}, u32[]{:S(2)}, u32[]{:S(2)}) collective-permute-start(f32[64,128]{1,0:T(8,128)} %get-tuple-element.14), channel_id=1, source_target_pairs={{0,1},{1,0},{2,3},{3,2},{4,5},{5,4},{6,7},{7,6},{8,9},{9,8},{10,11... | collective-permute-start | bytes 98312 | tf_op jit(solution)/shard_map/ppermute | solution.py:290

commit v4 on v3

--- a/solution.py
+++ b/solution.py
@@ -424,7 +424,7 @@
     held = spread(own)
     layout = tuple((mask, first) for mask, first, _ in held)
     vmem = pl.BlockSpec(memory_space=pltpu.VMEM)
-    hbm = pl.BlockSpec(memory_space=pl.ANY)
+    hbm = pl.BlockSpec(memory_space=pltpu.HBM)
     scale = 1.0 / (cells * planes * slabs)
     subspace, gram = pl.pallas_call(
         functools.partial(gram_kernel, layout=layout, scale=scale),

time: 69.9 us -> 69.9 us (level)
  no operation moved by 1% of the time
where the time goes in v4:
time: 69.9 us; the launch traced here: 69.3 us
  Pallas kernels  20.3 us (29%)
  starting transfers between devices  20.2 us (29%)
  waiting for transfers between devices  20.1 us (29%)
  local copies, waits for them, and re-layouts  5.25 us (8%)
  other arithmetic  2.69 us (4%)
  between operations  0.8 us (1%)
    ppermute x9, waiting for transfers between devices, swap(): return lax.ppermute(x, 'shift', [(i, i ^ mask) for i in range(count)])  11.8 us
    ppermute x6, starting transfers between devices, butterfly(): lax.ppermute(x, axis, [(i, i ^ m) for i in range(4)])  10.8 us
    pallas_call x1, Pallas kernels, on_device(): pl.pallas_call(krylov_kernel, grid_spec=pltpu.PrefetchScalarGridSpec(num_...  10.6 us
    ppermute x6, waiting for transfers between devices, butterfly(): lax.ppermute(x, axis, [(i, i ^ m) for i in range(4)])  6.81 us
    ppermute x9, starting transfers between devices, swap(): return lax.ppermute(x, 'shift', [(i, i ^ mask) for i in range(count)])  5.66 us
    pallas_call x1, Pallas kernels, on_device(): pl.pallas_call(moment_kernel, grid=((planes + 1) // group,), in_specs=[fu...  5.01 us
    pallas_call x1, Pallas kernels, on_device(): pl.pallas_call(functools.partial(gram_kernel, layout=layout, scale=scale)...  4.7 us
    ppermute x1, starting transfers between devices, on_device(): paired = lax.ppermute(edge(jnp.where(even, planes - 2, 0)), 'dom', pairs(0))  3.12 us
  transfers between devices with their start and end apart: 17, of which 10 were waited for; matrix products, arithmetic and copies ran while one was open for 1% of the time, Pallas kernels for 0%

profile of v4, /device:TPU:0, one launch (start us, length us, event | category | flops | bytes accessed | tf_op | source)
XLA Modules:
  0.0 69.3 jit_solution(15860108798132475278)
XLA Ops:
  0.7 0.8 %constant_dynamic-slice_fusion = (f32[2,1024]{1,0:T(2,128)S(1)}, f32[2,1024]{1,0:T(2,128)S(1)}) fusion(f32[8,1024]{1,0:T(8,128)} %pot.3, s32[]{:T(128)S(6)} %select_n.27, s32[]{:T(128)S(6)} %select_n.25), kind=kLoop, calls=%fused_computation.6 | loop fusion | bytes 32776 | tf_op jit(solution)/shard_map/dynamic_slice | solution.py:345
  1.5 0.9 %dynamic-slice_bitcast_fusion = (f32[16,1024]{1,0:T(8,128)S(1)}, f32[16,1024]{1,0:T(8,128)S(1)}) fusion(f32[8,64,1024]{2,1,0:T(8,128)} %own.1, s32[]{:T(128)S(6)} %select_n.27, s32[]{:T(128)S(6)} %select_n.26, s32[]{:T(128)S(6)} %select_n.25), kind=kLoop, calls=%fused_computation.2 | loop fusion | bytes 262156 | tf_op jit(solution)/shard_map/reshape | solution.py:346
  2.4 3.1 %collective-permute-start = (f32[18,1024]{1,0:T(8,128)S(1)}, f32[18,1024]{1,0:T(8,128)S(1)}, u32[]{:S(2)}, u32[]{:S(2)}) collective-permute-start(f32[18,1024]{1,0:T(8,128)S(1)} %pad_maximum_fusion), channel_id=1, source_target_pairs={{0,1},{2,3},{1,0},{3,2},{4,5},{6,7},{5,4},{7,6},{8,9},{10,11},{9,8... | collective-permute-start | bytes 221192 | tf_op jit(solution)/shard_map/ppermute | solution.py:353
  5.5 0.7 collective-permute-start.1
  6.2 0.6 pad_add_fusion.where
  6.8 1.5 %collective-permute-done.paired = f32[18,1024]{1,0:T(8,128)S(1)} collective-permute-done((f32[18,1024]{1,0:T(8,128)S(1)}, f32[18,1024]{1,0:T(8,128)S(1)}, u32[]{:S(2)}, u32[]{:S(2)}) %collective-permute-start) | collective-permute-done | bytes 73760 | tf_op jit(solution)/shard_map/ppermute | solution.py:353
  8.3 0.6 copy-done.9
  9.0 0.6 copy-done.10
  9.6 10.6 %krylov.1 = (f32[8,2,9,8,1024]{4,3,2,1,0:T(8,128)}, f32[12,8,1024]{2,1,0:T(8,128)}, f32[12,8,1024]{2,1,0:T(8,128)}, f32[8,128]{1,0:T(8,128)}) custom-call(s32[4]{0:T(128)} %pad_add_fusion.where, f32[8,2,128]{2,1,0:T(2,128)} %constant.42.clone.node, f32[8,64,1024]{2,1,0:T(8,128)} %own.1, f32[8,1024]{1,0:T(8,128)} %pot.3, f32[18,1024]{1,0:T(8,128)} %copy-done.9, ...), custom_call_target="tpu_custom_call" | custom-call | tf_op jit(solution)/shard_map/krylov/pallas_call | solution.py:368
  20.2 3.9 %collective-permute-start.4 = (f32[8,128]{1,0:T(8,128)}, f32[8,128]{1,0:T(8,128)S(1)}, u32[]{:S(2)}, u32[]{:S(2)}) collective-permute-start(f32[8,128]{1,0:T(8,128)} %get-tuple-element.12), channel_id=1, source_target_pairs={{0,3},{1,2},{2,1},{3,0},{4,7},{5,6},{6,5},{7,4},{8,11},{9,10},{10,... | collective-permute-start | bytes 12296 | tf_op jit(solution)/shard_map/ppermute | solution.py:290
  24.1 1.9 %collective-permute-start.3 = (f32[8,128]{1,0:T(8,128)}, f32[8,128]{1,0:T(8,128)S(1)}, u32[]{:S(2)}, u32[]{:S(2)}) collective-permute-start(f32[8,128]{1,0:T(8,128)} %get-tuple-element.12), channel_id=1, source_target_pairs={{0,2},{1,3},{2,0},{3,1},{4,6},{5,7},{6,4},{7,5},{8,10},{9,11},{10,... | collective-permute-start | bytes 12296 | tf_op jit(solution)/shard_map/ppermute | solution.py:290
  26.5 2.3 %collective-permute-done.3 = f32[8,128]{1,0:T(8,128)S(1)} collective-permute-done((f32[8,128]{1,0:T(8,128)}, f32[8,128]{1,0:T(8,128)S(1)}, u32[]{:S(2)}, u32[]{:S(2)}) %collective-permute-start.3) | collective-permute-done | bytes 4128 | tf_op jit(solution)/shard_map/ppermute | solution.py:290
  28.8 1.0 %collective-permute-done.2 = f32[8,128]{1,0:T(8,128)S(1)} collective-permute-done((f32[8,128]{1,0:T(8,128)}, f32[8,128]{1,0:T(8,128)S(1)}, u32[]{:S(2)}, u32[]{:S(2)}) %collective-permute-start.2) | collective-permute-done | bytes 4128 | tf_op jit(solution)/shard_map/ppermute | solution.py:290
  29.8 1.3 %add_add_fusion.1.sums = f32[8,128]{1,0:T(8,128)} fusion(f32[8,128]{1,0:T(8,128)S(1)} %collective-permute-done.3, f32[8,128]{1,0:T(8,128)S(1)} %collective-permute-done.4, f32[8,128]{1,0:T(8,128)} %get-tuple-element.12, f32[8,128]{1,0:T(8,128)S(1)} %collective-permute-done.2), kind=kLoop, calls=%fused_computation.5 | loop fusion | flops 3072 | bytes 20480 | tf_op jit(solution)/shard_map/add | solution.py:291
  31.1 5.0 %moment.1.refs_0_ = f32[9,8,1024]{2,1,0:T(8,128)} custom-call(f32[2,8,128]{2,1,0:T(8,128)} %constant.43.clone.shifts, f32[2,128]{1,0:T(2,128)} %constant.41.clone.weights, f32[8,2,9,8,1024]{4,3,2,1,0:T(8,128)} %get-tuple-element.9.blocks, f32[12,8,1024]{2,1,0:T(8,128)} %get-tuple-element.10.b_ref, f32[12,8,1024]{2,1,0:T(8,128)} %get-tuple-element.11.onsite, ...), custom_call_target="tpu_custom_call" | custom-call | tf_op jit(solution)/shard_map/moment/pallas_call | solution.py:405
  36.1 1.5 %collective-permute-start.6 = (f32[9,8,1024]{2,1,0:T(8,128)}, f32[9,8,1024]{2,1,0:T(8,128)S(1)}, u32[]{:S(2)}, u32[]{:S(2)}) collective-permute-start(f32[9,8,1024]{2,1,0:T(8,128)} %moment.1.refs_0_), channel_id=1, source_target_pairs={{0,16},{4,20},{8,24},{12,28},{16,0},{20,4},{24,8},{28,12},{1,17},{... | collective-permute-start | bytes 884744 | tf_op jit(solution)/shard_map/ppermute | solution.py:301
  37.6 1.5 %collective-permute-start.5 = (f32[9,8,1024]{2,1,0:T(8,128)}, f32[9,8,1024]{2,1,0:T(8,128)S(1)}, u32[]{:S(2)}, u32[]{:S(2)}) collective-permute-start(f32[9,8,1024]{2,1,0:T(8,128)} %moment.1.refs_0_), channel_id=1, source_target_pairs={{0,8},{4,12},{8,0},{12,4},{16,24},{20,28},{24,16},{28,20},{1,9},{5... | collective-permute-start | bytes 884744 | tf_op jit(solution)/shard_map/ppermute | solution.py:301
  39.1 3.9 %collective-permute-done.6.refs_2_ = f32[9,8,1024]{2,1,0:T(8,128)S(1)} collective-permute-done((f32[9,8,1024]{2,1,0:T(8,128)}, f32[9,8,1024]{2,1,0:T(8,128)S(1)}, u32[]{:S(2)}, u32[]{:S(2)}) %collective-permute-start.6) | collective-permute-done | bytes 294944 | tf_op jit(solution)/shard_map/ppermute | solution.py:301
  43.1 1.6 %collective-permute-start.8 = (f32[5,8,1024]{2,1,0:T(8,128)S(1)}, f32[5,8,1024]{2,1,0:T(8,128)S(1)}, u32[]{:S(2)}, u32[]{:S(2)}) collective-permute-start(f32[5,8,1024]{2,1,0:T(8,128)S(1)} %slice.17), channel_id=1, source_target_pairs={{0,8},{4,12},{8,0},{12,4},{16,24},{20,28},{24,16},{28,20},{1,9},{5... | collective-permute-start | bytes 491528 | tf_op jit(solution)/shard_map/ppermute | solution.py:301
  45.1 1.2 %collective-permute-done.5.refs_1_ = f32[9,8,1024]{2,1,0:T(8,128)S(1)} collective-permute-done((f32[9,8,1024]{2,1,0:T(8,128)}, f32[9,8,1024]{2,1,0:T(8,128)S(1)}, u32[]{:S(2)}, u32[]{:S(2)}) %collective-permute-start.5) | collective-permute-done | bytes 294944 | tf_op jit(solution)/shard_map/ppermute | solution.py:301
  46.3 0.6 collective-permute-start.7
  46.9 1.5 %collective-permute-done.8.refs_4_ = f32[5,8,1024]{2,1,0:T(8,128)S(1)} collective-permute-done((f32[5,8,1024]{2,1,0:T(8,128)S(1)}, f32[5,8,1024]{2,1,0:T(8,128)S(1)}, u32[]{:S(2)}, u32[]{:S(2)}) %collective-permute-start.8) | collective-permute-done | bytes 163872 | tf_op jit(solution)/shard_map/ppermute | solution.py:301
  48.5 3.9 %collective-permute-done.7.refs_3_ = f32[4,8,1024]{2,1,0:T(8,128)S(1)} collective-permute-done((f32[4,8,1024]{2,1,0:T(8,128)S(1)}, f32[4,8,1024]{2,1,0:T(8,128)S(1)}, u32[]{:S(2)}, u32[]{:S(2)}) %collective-permute-start.7) | collective-permute-done | bytes 131104 | tf_op jit(solution)/shard_map/ppermute | solution.py:301
  52.3 1.3 %collective-permute-done.12.refs_8_ = f32[4,8,1024]{2,1,0:T(8,128)S(1)} collective-permute-done((f32[4,8,1024]{2,1,0:T(8,128)S(1)}, f32[4,8,1024]{2,1,0:T(8,128)S(1)}, u32[]{:S(2)}, u32[]{:S(2)}) %collective-permute-start.12) | collective-permute-done | bytes 131104 | tf_op jit(solution)/shard_map/ppermute | solution.py:301
  54.6 0.7 copy-done.6
  55.2 4.7 %gram.1 = (f32[8,64,1024]{2,1,0:T(8,128)}, f32[64,128]{1,0:T(8,128)}) custom-call(s32[4]{0:T(128)} %pad_add_fusion.where, f32[8,1024]{1,0:T(8,128)} %pot.3, f32[9,8,1024]{2,1,0:T(8,128)} %moment.1.refs_0_, f32[9,8,1024]{2,1,0:T(8,128)} %copy-done.1, f32[9,8,1024]{2,1,0:T(8,128)} %copy-done, f32[4,8,1024]{2,1,0:T(8,128)} %copy-done.7, ...), custom_call_target="tpu_custom_call" | custom-call | tf_op jit(solution)/shard_map/gram/pallas_call | solution.py:429
  59.9 2.9 %collective-permute-start.16 = (f32[64,128]{1,0:T(8,128)}, f32[64,128]{1,0:T(8,128)S(1)}, u32[]{:S(2)}, u32[]{:S(2)}) collective-permute-start(f32[64,128]{1,0:T(8,128)} %get-tuple-element.14), channel_id=1, source_target_pairs={{0,3},{1,2},{2,1},{3,0},{4,7},{5,6},{6,5},{7,4},{8,11},{9,10},{10,... | collective-permute-start | bytes 98312 | tf_op jit(solution)/shard_map/ppermute | solution.py:290
  62.9 1.5 %collective-permute-start.14 = (f32[64,128]{1,0:T(8,128)}, f32[64,128]{1,0:T(8,128)S(1)}, u32[]{:S(2)}, u32[]{:S(2)}) collective-permute-start(f32[64,128]{1,0:T(8,128)} %get-tuple-element.14), channel_id=1, source_target_pairs={{0,1},{1,0},{2,3},{3,2},{4,5},{5,4},{6,7},{7,6},{8,9},{9,8},{10,11... | collective-permute-start | bytes 98312 | tf_op jit(solution)/shard_map/ppermute | solution.py:290
  64.4 1.6 %collective-permute-done.16 = f32[64,128]{1,0:T(8,128)S(1)} collective-permute-done((f32[64,128]{1,0:T(8,128)}, f32[64,128]{1,0:T(8,128)S(1)}, u32[]{:S(2)}, u32[]{:S(2)}) %collective-permute-start.16) | collective-permute-done | bytes 32800 | tf_op jit(solution)/shard_map/ppermute | solution.py:290
  66.0 1.8 %collective-permute-done.15 = f32[64,128]{1,0:T(8,128)S(1)} collective-permute-done((f32[64,128]{1,0:T(8,128)}, f32[64,128]{1,0:T(8,128)S(1)}, u32[]{:S(2)}, u32[]{:S(2)}) %collective-permute-start.15) | collective-permute-done | bytes 32800 | tf_op jit(solution)/shard_map/ppermute | solution.py:290
  67.9 0.8 %add_add_fusion = f32[64,128]{1,0:T(8,128)S(1)} fusion(f32[64,128]{1,0:T(8,128)S(1)} %collective-permute-done.15, f32[64,128]{1,0:T(8,128)S(1)} %collective-permute-done.16, f32[64,128]{1,0:T(8,128)} %get-tuple-element.14, f32[64,128]{1,0:T(8,128)S(1)} %collective-permute-done.14), kind=kLoop, calls=%fused_computation.4 | loop fusion | flops 24576 | bytes 163840 | tf_op jit(solution)/shard_map/add | solution.py:291
  68.7 0.7 %fusion = (f32[64,64]{1,0:T(8,128)}, f32[64,64]{1,0:T(8,128)}) fusion(f32[64,128]{1,0:T(8,128)S(1)} %add_add_fusion), kind=kLoop, calls=%fused_computation.9 | loop fusion | bytes 65536 | tf_op jit(solution)/shard_map/slice | solution.py:444
  (37 shorter events, 1.9 us)
Async XLA Ops:
  2.4 5.9 %collective-permute-start = (f32[18,1024]{1,0:T(8,128)S(1)}, f32[18,1024]{1,0:T(8,128)S(1)}, u32[]{:S(2)}, u32[]{:S(2)}) collective-permute-start(f32[18,1024]{1,0:T(8,128)S(1)} %pad_maximum_fusion), channel_id=1, source_target_pairs={{0,1},{2,3},{1,0},{3,2},{4,5},{6,7},{5,4},{7,6},{8,9},{10,11},{9,8... | collective-permute-start | bytes 221192 | tf_op jit(solution)/shard_map/ppermute | solution.py:353
  5.5 2.8 %collective-permute-start.1 = (f32[18,1024]{1,0:T(8,128)S(1)}, f32[18,1024]{1,0:T(8,128)S(1)}, u32[]{:S(2)}, u32[]{:S(2)}) collective-permute-start(f32[18,1024]{1,0:T(8,128)S(1)} %pad_maximum_fusion.1), channel_id=1, source_target_pairs={{1,2},{2,1},{5,6},{6,5},{9,10},{10,9},{13,14},{14,13},{17,18},{18,... | collective-permute-start | bytes 221192 | tf_op jit(solution)/shard_map/ppermute | solution.py:354
  8.3 0.7 copy-start.9
  9.0 0.6 copy-start.10
  20.2 6.3 %collective-permute-start.4 = (f32[8,128]{1,0:T(8,128)}, f32[8,128]{1,0:T(8,128)S(1)}, u32[]{:S(2)}, u32[]{:S(2)}) collective-permute-start(f32[8,128]{1,0:T(8,128)} %get-tuple-element.12), channel_id=1, source_target_pairs={{0,3},{1,2},{2,1},{3,0},{4,7},{5,6},{6,5},{7,4},{8,11},{9,10},{10,... | collective-permute-start | bytes 12296 | tf_op jit(solution)/shard_map/ppermute | solution.py:290
  24.1 4.7 %collective-permute-start.3 = (f32[8,128]{1,0:T(8,128)}, f32[8,128]{1,0:T(8,128)S(1)}, u32[]{:S(2)}, u32[]{:S(2)}) collective-permute-start(f32[8,128]{1,0:T(8,128)} %get-tuple-element.12), channel_id=1, source_target_pairs={{0,2},{1,3},{2,0},{3,1},{4,6},{5,7},{6,4},{7,5},{8,10},{9,11},{10,... | collective-permute-start | bytes 12296 | tf_op jit(solution)/shard_map/ppermute | solution.py:290
  26.0 3.8 %collective-permute-start.2 = (f32[8,128]{1,0:T(8,128)}, f32[8,128]{1,0:T(8,128)S(1)}, u32[]{:S(2)}, u32[]{:S(2)}) collective-permute-start(f32[8,128]{1,0:T(8,128)} %get-tuple-element.12), channel_id=1, source_target_pairs={{0,1},{1,0},{2,3},{3,2},{4,5},{5,4},{6,7},{7,6},{8,9},{9,8},{10,11... | collective-permute-start | bytes 12296 | tf_op jit(solution)/shard_map/ppermute | solution.py:290
  36.1 6.9 %collective-permute-start.6 = (f32[9,8,1024]{2,1,0:T(8,128)}, f32[9,8,1024]{2,1,0:T(8,128)S(1)}, u32[]{:S(2)}, u32[]{:S(2)}) collective-permute-start(f32[9,8,1024]{2,1,0:T(8,128)} %moment.1.refs_0_), channel_id=1, source_target_pairs={{0,16},{4,20},{8,24},{12,28},{16,0},{20,4},{24,8},{28,12},{1,17},{... | collective-permute-start | bytes 884744 | tf_op jit(solution)/shard_map/ppermute | solution.py:301
  37.6 8.7 %collective-permute-start.5 = (f32[9,8,1024]{2,1,0:T(8,128)}, f32[9,8,1024]{2,1,0:T(8,128)S(1)}, u32[]{:S(2)}, u32[]{:S(2)}) collective-permute-start(f32[9,8,1024]{2,1,0:T(8,128)} %moment.1.refs_0_), channel_id=1, source_target_pairs={{0,8},{4,12},{8,0},{12,4},{16,24},{20,28},{24,16},{28,20},{1,9},{5... | collective-permute-start | bytes 884744 | tf_op jit(solution)/shard_map/ppermute | solution.py:301
  43.1 10.7 %copy-start = (f32[9,8,1024]{2,1,0:T(8,128)}, f32[9,8,1024]{2,1,0:T(8,128)S(1)}, u32[]{:S(2)}) copy-start(f32[9,8,1024]{2,1,0:T(8,128)S(1)} %collective-permute-done.6.refs_2_) | copy-start | bytes 884740
  43.1 5.4 %collective-permute-start.8 = (f32[5,8,1024]{2,1,0:T(8,128)S(1)}, f32[5,8,1024]{2,1,0:T(8,128)S(1)}, u32[]{:S(2)}, u32[]{:S(2)}) collective-permute-start(f32[5,8,1024]{2,1,0:T(8,128)S(1)} %slice.17), channel_id=1, source_target_pairs={{0,8},{4,12},{8,0},{12,4},{16,24},{20,28},{24,16},{28,20},{1,9},{5... | collective-permute-start | bytes 491528 | tf_op jit(solution)/shard_map/ppermute | solution.py:301
  44.6 7.7 %collective-permute-start.9 = (f32[9,8,1024]{2,1,0:T(8,128)}, f32[9,8,1024]{2,1,0:T(8,128)S(1)}, u32[]{:S(2)}, u32[]{:S(2)}) collective-permute-start(f32[9,8,1024]{2,1,0:T(8,128)} %moment.1.refs_0_), channel_id=1, source_target_pairs={{0,4},{4,0},{8,12},{12,8},{16,20},{20,16},{24,28},{28,24},{1,5},{5... | collective-permute-start | bytes 884744 | tf_op jit(solution)/shard_map/ppermute | solution.py:301
  44.6 9.0 %collective-permute-start.11 = (f32[9,8,1024]{2,1,0:T(8,128)S(1)}, f32[9,8,1024]{2,1,0:T(8,128)S(1)}, u32[]{:S(2)}, u32[]{:S(2)}) collective-permute-start(f32[9,8,1024]{2,1,0:T(8,128)S(1)} %collective-permute-done.6.refs_2_), channel_id=1, source_target_pairs={{0,4},{4,0},{8,12},{12,8},{16,20},{20,16},{24,28},{28,24},{1,5},{5... | collective-permute-start | bytes 884744 | tf_op jit(solution)/shard_map/ppermute | solution.py:301
  46.3 7.4 %copy-start.1 = (f32[9,8,1024]{2,1,0:T(8,128)}, f32[9,8,1024]{2,1,0:T(8,128)S(1)}, u32[]{:S(2)}) copy-start(f32[9,8,1024]{2,1,0:T(8,128)S(1)} %collective-permute-done.5.refs_1_) | copy-start | bytes 884740
  46.3 7.4 %collective-permute-start.10 = (f32[9,8,1024]{2,1,0:T(8,128)S(1)}, f32[9,8,1024]{2,1,0:T(8,128)S(1)}, u32[]{:S(2)}, u32[]{:S(2)}) collective-permute-start(f32[9,8,1024]{2,1,0:T(8,128)S(1)} %collective-permute-done.5.refs_1_), channel_id=1, source_target_pairs={{0,4},{4,0},{8,12},{12,8},{16,20},{20,16},{24,28},{28,24},{1,5},{5... | collective-permute-start | bytes 884744 | tf_op jit(solution)/shard_map/ppermute | solution.py:301
  46.3 6.0 %collective-permute-start.7 = (f32[4,8,1024]{2,1,0:T(8,128)S(1)}, f32[4,8,1024]{2,1,0:T(8,128)S(1)}, u32[]{:S(2)}, u32[]{:S(2)}) collective-permute-start(f32[4,8,1024]{2,1,0:T(8,128)S(1)} %slice.16), channel_id=1, source_target_pairs={{0,16},{4,20},{8,24},{12,28},{16,0},{20,4},{24,8},{28,12},{1,17},{... | collective-permute-start | bytes 393224 | tf_op jit(solution)/shard_map/ppermute | solution.py:301
  48.5 5.3 %copy-start.5 = (f32[5,8,1024]{2,1,0:T(8,128)}, f32[5,8,1024]{2,1,0:T(8,128)S(1)}, u32[]{:S(2)}) copy-start(f32[5,8,1024]{2,1,0:T(8,128)S(1)} %collective-permute-done.8.refs_4_) | copy-start | bytes 491524
  48.5 5.2 %collective-permute-start.13 = (f32[5,8,1024]{2,1,0:T(8,128)S(1)}, f32[5,8,1024]{2,1,0:T(8,128)S(1)}, u32[]{:S(2)}, u32[]{:S(2)}) collective-permute-start(f32[5,8,1024]{2,1,0:T(8,128)S(1)} %collective-permute-done.8.refs_4_), channel_id=1, source_target_pairs={{0,4},{4,0},{8,12},{12,8},{16,20},{20,16},{24,28},{28,24},{1,5},{5... | collective-permute-start | bytes 491528 | tf_op jit(solution)/shard_map/ppermute | solution.py:301
  52.3 1.4 %copy-start.7 = (f32[4,8,1024]{2,1,0:T(8,128)}, f32[4,8,1024]{2,1,0:T(8,128)S(1)}, u32[]{:S(2)}) copy-start(f32[4,8,1024]{2,1,0:T(8,128)S(1)} %collective-permute-done.7.refs_3_) | copy-start | bytes 393220
  52.3 1.3 %collective-permute-start.12 = (f32[4,8,1024]{2,1,0:T(8,128)S(1)}, f32[4,8,1024]{2,1,0:T(8,128)S(1)}, u32[]{:S(2)}, u32[]{:S(2)}) collective-permute-start(f32[4,8,1024]{2,1,0:T(8,128)S(1)} %collective-permute-done.7.refs_3_), channel_id=1, source_target_pairs={{0,4},{4,0},{8,12},{12,8},{16,20},{20,16},{24,28},{28,24},{1,5},{5... | collective-permute-start | bytes 393224 | tf_op jit(solution)/shard_map/ppermute | solution.py:301
  52.3 1.4 %copy-start.2 = (f32[9,8,1024]{2,1,0:T(8,128)}, f32[9,8,1024]{2,1,0:T(8,128)S(1)}, u32[]{:S(2)}) copy-start(f32[9,8,1024]{2,1,0:T(8,128)S(1)} %collective-permute-done.9.refs_5_) | copy-start | bytes 884740
  53.7 0.7 copy-start.8
  53.7 0.8 %copy-start.3 = (f32[9,8,1024]{2,1,0:T(8,128)}, f32[9,8,1024]{2,1,0:T(8,128)S(1)}, u32[]{:S(2)}) copy-start(f32[9,8,1024]{2,1,0:T(8,128)S(1)} %collective-permute-done.11.refs_7_) | copy-start | bytes 884740
  53.7 0.9 %copy-start.4 = (f32[9,8,1024]{2,1,0:T(8,128)}, f32[9,8,1024]{2,1,0:T(8,128)S(1)}, u32[]{:S(2)}) copy-start(f32[9,8,1024]{2,1,0:T(8,128)S(1)} %collective-permute-done.10.refs_6_) | copy-start | bytes 884740
  54.6 0.7 copy-start.6
  59.9 6.1 %collective-permute-start.16 = (f32[64,128]{1,0:T(8,128)}, f32[64,128]{1,0:T(8,128)S(1)}, u32[]{:S(2)}, u32[]{:S(2)}) collective-permute-start(f32[64,128]{1,0:T(8,128)} %get-tuple-element.14), channel_id=1, source_target_pairs={{0,3},{1,2},{2,1},{3,0},{4,7},{5,6},{6,5},{7,4},{8,11},{9,10},{10,... | collective-permute-start | bytes 98312 | tf_op jit(solution)/shard_map/ppermute | solution.py:290
  62.9 5.0 %collective-permute-start.15 = (f32[64,128]{1,0:T(8,128)}, f32[64,128]{1,0:T(8,128)S(1)}, u32[]{:S(2)}, u32[]{:S(2)}) collective-permute-start(f32[64,128]{1,0:T(8,128)} %get-tuple-element.14), channel_id=1, source_target_pairs={{0,2},{1,3},{2,0},{3,1},{4,6},{5,7},{6,4},{7,5},{8,10},{9,11},{10,... | collective-permute-start | bytes 98312 | tf_op jit(solution)/shard_map/ppermute | solution.py:290
  62.9 5.0 %collective-permute-start.14 = (f32[64,128]{1,0:T(8,128)}, f32[64,128]{1,0:T(8,128)S(1)}, u32[]{:S(2)}, u32[]{:S(2)}) collective-permute-start(f32[64,128]{1,0:T(8,128)} %get-tuple-element.14), channel_id=1, source_target_pairs={{0,1},{1,0},{2,3},{3,2},{4,5},{5,4},{6,7},{7,6},{8,9},{9,8},{10,11... | collective-permute-start | bytes 98312 | tf_op jit(solution)/shard_map/ppermute | solution.py:290
